TPU v7x, 32 devices: a whole 2x2x4 slice. The times are simulated.
32 devices in a mesh: rep: 2 (over y), span: 2 (over core), seq: 4 (over z), tp: 2 (over x).
Axes of the slice: x: 2, y: 2, z: 4, core: 2. Of those that a mesh axis runs over, the one named last changes fastest.
Arguments:
- queries: bfloat16 [8, 512, 24, 128], P(('rep', 'span'), 'seq', 'tp'), parts along dimension 0, may hold values from -110 to 110
- key_states: bfloat16 [8, 512, 4, 128], P(('rep', 'span'), 'seq', 'tp'), parts along dimension 0, may hold values from -11 to 11
- value_states: bfloat16 [8, 512, 4, 128], P(('rep', 'span'), 'seq', 'tp'), parts along dimension 0, may hold values from -6 to 6
- out_weight: bfloat16 [3072, 6144], P('tp', 'seq'), may hold values from -0.109375 to 0.109375
- noise_table: float32 [64, 6144], P(None, 'tp'), may hold values from 0.5 to 2
- plan: int32 [8], P('rep'), parts along dimension 0, may hold values from 0 to 63
Outputs:
- branch_out: bfloat16 [8, 512, 6144], P(('rep', 'span'), 'seq', 'tp'), parts along dimension 0
There are 2 independent parts, one for each index of `rep`. A program takes and returns all parts, laid end to end along the dimension named above; an argument that names none is the same for every part. Nothing has to cross between parts.
All inputs are finite; a program needn't handle non-finite values.
Results may differ from a plain program's by a relative error of at most 0.014.
Values may be sent and summed in bfloat16 or wider, within the bound.
A program may use at most 128 MiB of HBM per device.

v0:
```python
import functools
import math

import jax
import jax.numpy as jnp
from jax import lax
from jax.experimental import pallas as pl
from jax.experimental.pallas import tpu as pltpu
from jax.sharding import PartitionSpec as P

MESH = pl.DeviceIdType.MESH


def fused_kernel(
    parts, plan_ref, q_ref, kv_ref, noise_ref, w_ref, out_ref,
    kvbuf, wbuf, abuf, pbuf, xsend, xbuf,
    kv_send, kv_recv, kvc, loc, wz_send, wc_send, wy_send,
    wz_recv, wc_recv, wy_recv, x_send, x_recv,
):
    y, c = lax.axis_index("rep"), lax.axis_index("span")
    z, t = lax.axis_index("seq"), lax.axis_index("tp")
    n = lax.axis_size("seq")
    cores, tps = lax.axis_size("span"), lax.axis_size("tp")
    spans, heads, tok, hd = q_ref.shape
    kvh = kv_ref.shape[1]
    per_kv = heads // kvh
    depth, cols = w_ref.shape
    quarter = depth // (cores * lax.axis_size("rep"))
    sub = cols // parts
    owned = n // tps
    first = c * spans
    steps = (n - 1) * parts
    scale = hd ** (-0.5) * math.log2(math.e)

    def rows(yy, cc):
        return pl.ds(pl.multiple_of((yy * cores + cc) * quarter, quarter), quarter)

    def remote(src, dst, send, recv, where):
        return pltpu.make_async_remote_copy(
            src_ref=src, dst_ref=dst, send_sem=send, recv_sem=recv,
            device_id=where, device_id_type=MESH,
        )

    def z_copy(s, j, way, own):
        dst = wbuf.at[s, j, rows(y, c)]
        src = w_ref.at[rows(y, c), pl.ds(pl.multiple_of(j * sub, sub), sub)] if own else dst
        to = z - 1 if way == 0 else z + 1
        return remote(src, dst, wz_send.at[way, s, j], wz_recv.at[s, j], {"seq": to})

    def core_copy(s, j, kind):
        part = wbuf.at[s, j, rows(y if kind == 0 else 1 - y, c)]
        return remote(part, part, wc_send.at[kind, s, j], wc_recv.at[kind, s, j], {"span": 1 - c})

    def y_copy(s, j):
        part = wbuf.at[s, j, rows(y, c)]
        return remote(part, part, wy_send.at[s, j], wy_recv.at[s, j], {"rep": 1 - y})

    def x_copy(s, j):
        at = lax.rem(s, owned)
        return remote(xsend.at[at, j], xbuf.at[at, j], x_send.at[at, j], x_recv.at[at, j], {"tp": 1 - t})

    def kv_copy(to, at):
        return remote(
            kv_ref, kvbuf.at[pl.ds(first, spans), :, :, z], kv_send.at[to], kv_recv.at[at], {"seq": to}
        )

    def kv_core():
        part = kvbuf.at[pl.ds(0, spans)]
        return remote(part, part, kvc.at[0], kvc.at[1], {"span": 1 - c})

    def local_w(j):
        return pltpu.make_async_copy(
            w_ref.at[:, pl.ds(pl.multiple_of(j * sub, sub), sub)], wbuf.at[z, j], loc.at[j]
        )

    def local_kv():
        return pltpu.make_async_copy(
            kv_ref, kvbuf.at[pl.ds(first, spans), :, :, z], loc.at[parts]
        )

    barrier = pltpu.get_barrier_semaphore()
    for peer in range(n):
        @pl.when(z != peer)
        def _(peer=peer):
            pl.semaphore_signal(barrier, inc=1, device_id={"seq": peer}, device_id_type=MESH)
    pl.semaphore_signal(barrier, inc=1, device_id={"rep": 1 - y}, device_id_type=MESH)
    pl.semaphore_signal(barrier, inc=1, device_id={"span": 1 - c}, device_id_type=MESH)
    pl.semaphore_signal(barrier, inc=1, device_id={"tp": 1 - t}, device_id_type=MESH)
    pl.semaphore_wait(barrier, n - 1 + 3)

    local_kv().start()
    for peer in range(n):
        @pl.when(z != peer)
        def _(peer=peer):
            kv_copy(peer, z).start()
    for j in range(parts):
        @pl.when(z > 0)
        def _(j=j):
            z_copy(z, j, 0, True).start()

        @pl.when(z < n - 1)
        def _(j=j):
            z_copy(z, j, 1, True).start()
    for j in range(parts):
        local_w(j).start()

    local_kv().wait()
    for peer in range(n):
        @pl.when(z != peer)
        def _(peer=peer):
            kv_copy(peer, peer).wait_recv()

    @pl.when(c == 0)
    def _():
        kv_core().start()

    @pl.when(c != 0)
    def _():
        kv_core().wait_recv()

    def each(e, low, do):
        ok = jnp.logical_and(e >= low, e < steps)
        d, j = e // parts + 1, e % parts
        for sign in (-1, 1):
            s = z + sign * d

            @pl.when(jnp.logical_and(ok, jnp.logical_and(s >= 0, s < n)))
            def _(s=s, sign=sign):
                do(s, j, sign)

    def arrive(s, j, sign):
        way = 0 if sign > 0 else 1
        z_copy(s, j, way, False).wait_recv()

        @pl.when((z > 0) if way == 0 else (z < n - 1))
        def _():
            z_copy(s, j, way, False).start()

        y_copy(s, j).start()
        core_copy(s, j, 0).start()

    def pass_on(s, j, sign):
        y_copy(s, j).wait_recv()
        core_copy(s, j, 1).start()

    def project(s, j):
        part = jnp.dot(abuf[...], wbuf[s, j], preferred_element_type=jnp.float32)
        at = lax.rem(s, owned)

        @pl.when(s // owned == t)
        def _():
            pbuf[at, j] = part

        @pl.when(s // owned != t)
        def _():
            xsend[at, j] = part.astype(jnp.bfloat16)
            x_copy(s, j).start()

    def gather_project(s, j, sign):
        core_copy(s, j, 0).wait_recv()
        core_copy(s, j, 1).wait_recv()
        project(s, j)

    def finish(s, j, sign):
        @pl.when(s // owned == t)
        def _():
            x_copy(s, j).wait_recv()
            at = lax.rem(s, owned)
            where = pl.ds(pl.multiple_of(at * cols + j * sub, 128), sub)
            for i in range(spans):
                level = plan_ref[first + i]
                gate = noise_ref[pl.ds(level, 1), where]
                mine = pl.ds(i * tok, tok)
                total = pbuf[at, j, mine, :] + xbuf[at, j, mine, :].astype(jnp.float32)
                out_ref[mine, where] = (total * gate).astype(out_ref.dtype)

    units = spans * kvh
    lag = units - 1
    lead = per_kv * tok

    def attend(u, carry):
        i, g = u // kvh, u % kvh
        query = q_ref[i, pl.ds(g * per_kv, per_kv)].reshape(lead, hd)

        def fold(k, state):
            top, total, mixed = state
            keys = kvbuf[k, g, 0].reshape(n * tok, hd)
            values = kvbuf[k, g, 1].reshape(n * tok, hd)
            scores = lax.dot_general(
                query, keys, (((1,), (1,)), ((), ())), preferred_element_type=jnp.float32
            )
            high = jnp.maximum(top, jnp.max(scores, axis=1, keepdims=True))
            shrink = jnp.exp2((top - high) * scale)
            weights = jnp.exp2((scores - high) * scale)
            total = total * shrink + jnp.sum(weights, axis=1, keepdims=True)
            mixed = mixed * shrink + jnp.dot(
                weights.astype(jnp.bfloat16), values, preferred_element_type=jnp.float32
            )
            return high, total, mixed

        start = (
            jnp.full((lead, 1), -1e30, jnp.float32),
            jnp.zeros((lead, 1), jnp.float32),
            jnp.zeros((lead, hd), jnp.float32),
        )
        _, total, mixed = lax.fori_loop(0, first + i + 1, fold, start)
        result = (mixed / total).astype(jnp.bfloat16).reshape(per_kv, tok, hd)
        for h in range(per_kv):
            abuf[
                pl.ds(pl.multiple_of(i * tok, tok), tok),
                pl.ds(pl.multiple_of((g * per_kv + h) * hd, hd), hd),
            ] = result[h]
        each(u, 0, arrive)
        each(u - lag, 0, pass_on)
        return carry

    lax.fori_loop(0, units, attend, 0)

    def own(j, carry):
        local_w(j).wait()
        project(z, j)
        return carry

    lax.fori_loop(0, parts, own, 0)

    def run(e, carry):
        each(e, units, arrive)
        each(e - lag, units - lag, pass_on)
        each(e - lag - 1, 0, gather_project)
        each(e - lag - 3, 0, finish)
        return carry

    lax.fori_loop(0, parts, lambda j, carry: (finish(z, j, 0), carry)[1], 0)
    lax.fori_loop(units, max(steps, units) + lag + 3, run, 0)

    for peer in range(n):
        @pl.when(z != peer)
        def _(peer=peer):
            kv_copy(peer, z).wait_send()

    @pl.when(c == 0)
    def _():
        kv_core().wait_send()

    def drain(f, carry):
        s, j = f // parts, f % parts

        @pl.when(jnp.logical_and(z > 0, s >= z))
        def _():
            z_copy(s, j, 0, False).wait_send()

        @pl.when(jnp.logical_and(z < n - 1, s <= z))
        def _():
            z_copy(s, j, 1, False).wait_send()

        @pl.when(s != z)
        def _():
            core_copy(s, j, 0).wait_send()
            core_copy(s, j, 1).wait_send()
            y_copy(s, j).wait_send()

        @pl.when(s // owned != t)
        def _():
            x_copy(s, j).wait_send()

        return carry

    lax.fori_loop(0, n * parts, drain, 0)


def fused(parts, queries, key_states, value_states, out_weight, noise_table, plan):
    spans, tok, heads, hd = queries.shape
    kvh = key_states.shape[2]
    depth, cols = out_weight.shape
    n, tps, cores = lax.axis_size("seq"), lax.axis_size("tp"), lax.axis_size("span")
    sub, owned, wide = cols // parts, n // tps, noise_table.shape[1]
    q = jnp.transpose(queries, (0, 2, 1, 3))
    kv = jnp.stack([key_states, value_states], axis=0).transpose(1, 3, 0, 2, 4)
    vmem = pl.BlockSpec(memory_space=pltpu.VMEM)
    dma = pltpu.SemaphoreType.DMA
    out = pl.pallas_call(
        functools.partial(fused_kernel, parts),
        out_shape=jax.ShapeDtypeStruct((spans * tok, wide), jnp.bfloat16),
        in_specs=[
            pl.BlockSpec(memory_space=pltpu.SMEM), vmem, vmem, vmem,
            pl.BlockSpec(memory_space=pl.ANY),
        ],
        out_specs=vmem,
        scratch_shapes=[
            pltpu.VMEM((spans * cores, kvh, 2, n, tok, hd), jnp.bfloat16),
            pltpu.VMEM((n, parts, depth, sub), jnp.bfloat16),
            pltpu.VMEM((spans * tok, depth), jnp.bfloat16),
            pltpu.VMEM((owned, parts, spans * tok, sub), jnp.float32),
            pltpu.VMEM((owned, parts, spans * tok, sub), jnp.bfloat16),
            pltpu.VMEM((owned, parts, spans * tok, sub), jnp.bfloat16),
            dma((n,)), dma((n,)), dma((2,)), dma((parts + 1,)),
            dma((2, n, parts)), dma((2, n, parts)), dma((n, parts)),
            dma((n, parts)), dma((2, n, parts)), dma((n, parts)),
            dma((owned, parts)), dma((owned, parts)),
        ],
        compiler_params=pltpu.CompilerParams(
            collective_id=0, has_side_effects=True, vmem_limit_bytes=60 * 1024 * 1024
        ),
        name="relay_attention",
    )(plan, q, kv, noise_table, out_weight)
    return out.reshape(spans, tok, wide)


def fold_block(carried, query_rows, key_rows, value_rows, factor):
    maxima, totals, weighted = carried
    scores = (
        jnp.einsum("tkgd,skd->tkgs", query_rows, key_rows, preferred_element_type=jnp.float32)
        * factor
    )
    highest = jnp.maximum(maxima, jnp.max(scores, axis=-1))
    shrink = jnp.exp(maxima - highest)
    weights = jnp.exp(scores - highest[..., None])
    totals = totals * shrink + jnp.sum(weights, axis=-1)
    weighted = weighted * shrink[..., None] + jnp.einsum(
        "tkgs,skd->tkgd",
        weights.astype(jnp.bfloat16),
        value_rows,
        preferred_element_type=jnp.float32,
    )
    return (maxima * 0.0 + highest, totals, weighted)


def per_device(queries, key_states, value_states, out_weight, noise_table, plan):
    ch_dev, tok_dev, heads_local, head_size = queries.shape
    kv_local = key_states.shape[2]
    per_kv = heads_local // kv_local
    span_count = ch_dev * lax.axis_size("span")
    first_span = lax.axis_index("span") * ch_dev
    factor = head_size ** (-0.5)
    grouped = queries.reshape(ch_dev, tok_dev, kv_local, per_kv, head_size)
    start_max = jnp.full((ch_dev, tok_dev, kv_local, per_kv), -1e30, jnp.float32)
    start_tot = jnp.zeros((ch_dev, tok_dev, kv_local, per_kv), jnp.float32)
    start_acc = jnp.zeros((ch_dev, tok_dev, kv_local, per_kv, head_size), jnp.float32)
    span_rows = (
        lax.all_gather(key_states, "seq", axis=1, tiled=True),
        lax.all_gather(value_states, "seq", axis=1, tiled=True),
    )
    key_piece = lax.all_gather(span_rows[0], "span", axis=0, tiled=True)
    value_piece = lax.all_gather(span_rows[1], "span", axis=0, tiled=True)
    new_max = []
    new_tot = []
    new_acc = []
    for q_span in range(ch_dev):
        inner_state = (start_max[q_span], start_tot[q_span], start_acc[q_span])
        for k_span in range(span_count):

            def update(inner, q_span=q_span, k_span=k_span):
                return fold_block(
                    inner, grouped[q_span], key_piece[k_span], value_piece[k_span], factor
                )

            inner_state = lax.cond(
                k_span <= first_span + q_span, update, lambda inner: inner, inner_state
            )
        new_max.append(inner_state[0])
        new_tot.append(inner_state[1])
        new_acc.append(inner_state[2])
    attn = (
        (jnp.stack(new_acc) / jnp.stack(new_tot)[..., None])
        .reshape(ch_dev, tok_dev, heads_local * head_size)
        .astype(jnp.bfloat16)
    )
    columns = jnp.einsum(
        "ctf,fo->cto",
        lax.all_gather(attn, "seq", axis=1, tiled=True),
        out_weight,
        preferred_element_type=jnp.float32,
    )
    partial_out = lax.all_to_all(
        columns.astype(jnp.bfloat16), "seq", split_axis=1, concat_axis=2, tiled=True
    ).astype(columns.dtype)
    summed = lax.psum_scatter(
        partial_out.astype(jnp.bfloat16), "tp", scatter_dimension=2, tiled=True
    ).astype(jnp.float32)
    levels = lax.dynamic_slice_in_dim(plan, first_span, ch_dev)
    picks = (levels[:, None] == jnp.arange(noise_table.shape[0], dtype=jnp.int32)[None, :]).astype(
        jnp.float32
    )
    gates = jnp.dot(picks, noise_table, precision=lax.Precision.HIGHEST)
    return (summed * gates[:, None, :]).astype(jnp.bfloat16)


def choose_parts(cols):
    for parts in (6, 3, 2, 1):
        if cols % (parts * 128) == 0:
            return parts
    return 0


def dispatch(queries, key_states, value_states, out_weight, noise_table, plan):
    depth, cols = out_weight.shape
    copies = lax.axis_size("rep") * lax.axis_size("span")
    parts = choose_parts(cols)
    pairs = all(lax.axis_size(name) == 2 for name in ("rep", "span", "tp"))
    args = (queries, key_states, value_states, out_weight, noise_table, plan)
    if pairs and parts and depth % (copies * 16) == 0 and lax.axis_size("seq") % 2 == 0:
        return fused(parts, *args)
    return per_device(*args)


def solution(mesh):
    placed = (
        P(("rep", "span"), "seq", "tp", None),
        P(("rep", "span"), "seq", "tp", None),
        P(("rep", "span"), "seq", "tp", None),
        P("tp", "seq"),
        P(None, "tp"),
        P("rep"),
    )
    return jax.shard_map(
        dispatch,
        mesh=mesh,
        in_specs=placed,
        out_specs=P(("rep", "span"), "seq", "tp"),
        check_vma=False,
    )
```

profile of v0, /device:TPU:2, one launch (start us, length us, event | category | flops | bytes accessed | tf_op | source)
XLA Modules:
  0.0 136.2 jit_solution(5738295177670229224)
XLA Ops:
  0.0 1.0 copy_bitcast_fusion
  1.0 0.7 maximum_bitcast_fusion.kv_ref
  1.7 131.8 %relay_attention.1 = bf16[256,3072]{1,0:T(8,128)(2,1)} custom-call(s32[4]{0:T(128)} %plan_ref.1, bf16[2,12,128,128]{3,2,1,0:T(8,128)(2,1)} %bitcast.9, bf16[2,2,2,128,128]{4,3,2,1,0:T(8,128)(2,1)} %maximum_bitcast_fusion.kv_ref, f32[64,3072]{1,0:T(8,128)} %noise_ref.1, bf16[1536,1536]{1,0:T(8,128)(2,1)} %w_ref.1), custom_call_target="tpu_custom_call" | custom-call | tf_op jit(solution)/shard_map/relay_attention/pallas_call | solution.py:281
  133.5 2.7 %copy.12 = bf16[2,128,3072]{2,1,0:T(8,128)(2,1)} copy(bf16[2,128,3072]{2,1,0:T(8,128)(2,1)} %bitcast.8) | data formatting | bytes 3145728
where the time goes:
time: 137 us; the launch traced here: 136 us
  Pallas kernels  132 us (96%)
  local copies, waits for them, and re-layouts  3.65 us (3%)
    pallas_call x1, Pallas kernels, fused(): pl.pallas_call(functools.partial(fused_kernel, parts), out_shape=jax.Shap...  132 us

commit v1 on v0

--- a/solution.py
+++ b/solution.py
@@ -12,10 +12,10 @@
 
 
 def fused_kernel(
-    parts, plan_ref, q_ref, kv_ref, noise_ref, w_ref, out_ref,
-    kvbuf, wbuf, abuf, pbuf, xsend, xbuf,
-    kv_send, kv_recv, kvc, loc, wz_send, wc_send, wy_send,
-    wz_recv, wc_recv, wy_recv, x_send, x_recv,
+    parts, keep, late, plan_ref, q_ref, kv_ref, noise_ref, w_ref, out_ref,
+    kvbuf, wbuf, abuf, pbuf, xsend, xbuf, csend, cbuf,
+    kv_send, kv_recv, kvc_send, kvc_recv, loc, wz_send, wz_recv, wf_send, wf_recv,
+    wc_send, wc_recv, wy_send, wy_recv, x_send, x_recv, a_send, a_recv, c_send, c_recv,
 ):
     y, c = lax.axis_index("rep"), lax.axis_index("span")
     z, t = lax.axis_index("seq"), lax.axis_index("tp")
@@ -28,12 +28,30 @@
     quarter = depth // (cores * lax.axis_size("rep"))
     sub = cols // parts
     owned = n // tps
+    rows_own = spans * tok
     first = c * spans
-    steps = (n - 1) * parts
+    last = n - 1
+    steps = last * parts
     scale = hd ** (-0.5) * math.log2(math.e)
+    both = jnp.logical_and
+
+    is_end = jnp.logical_or(z == 0, z == last)
+    inward = jnp.where(2 * z < n, 1, -1)
+    is_host = jnp.logical_or(z == 1, z == n - 2)
+    guest = z - inward
+
+    def wanted(r, s, j):
+        far = (jnp.abs(s - r) - 1) * parts + j >= keep
+        return jnp.logical_not(both(jnp.logical_or(r == 0, r == last), far))
+
+    def whole(s, j):
+        return both(is_host, both(s == guest, j >= late))
 
     def rows(yy, cc):
         return pl.ds(pl.multiple_of((yy * cores + cc) * quarter, quarter), quarter)
+
+    def columns(j):
+        return pl.ds(pl.multiple_of(j * sub, sub), sub)
 
     def remote(src, dst, send, recv, where):
         return pltpu.make_async_remote_copy(
@@ -43,9 +61,15 @@
 
     def z_copy(s, j, way, own):
         dst = wbuf.at[s, j, rows(y, c)]
-        src = w_ref.at[rows(y, c), pl.ds(pl.multiple_of(j * sub, sub), sub)] if own else dst
+        src = w_ref.at[rows(y, c), columns(j)] if own else dst
         to = z - 1 if way == 0 else z + 1
         return remote(src, dst, wz_send.at[way, s, j], wz_recv.at[s, j], {"seq": to})
+
+    def rest_copy(s, j):
+        src = w_ref.at[rows(1 - y, c), columns(j)]
+        return remote(
+            src, wbuf.at[s, j, rows(1 - y, c)], wf_send.at[j], wf_recv.at[j], {"seq": z + inward}
+        )
 
     def core_copy(s, j, kind):
         part = wbuf.at[s, j, rows(y if kind == 0 else 1 - y, c)]
@@ -55,96 +79,141 @@
         part = wbuf.at[s, j, rows(y, c)]
         return remote(part, part, wy_send.at[s, j], wy_recv.at[s, j], {"rep": 1 - y})
 
-    def x_copy(s, j):
+    def x_copy(s, j, src):
         at = lax.rem(s, owned)
-        return remote(xsend.at[at, j], xbuf.at[at, j], x_send.at[at, j], x_recv.at[at, j], {"tp": 1 - t})
-
-    def kv_copy(to, at):
         return remote(
-            kv_ref, kvbuf.at[pl.ds(first, spans), :, :, z], kv_send.at[to], kv_recv.at[at], {"seq": to}
-        )
-
-    def kv_core():
-        part = kvbuf.at[pl.ds(0, spans)]
-        return remote(part, part, kvc.at[0], kvc.at[1], {"span": 1 - c})
+            src.at[at, j], xbuf.at[at, j], x_send.at[at, j], x_recv.at[at, j], {"tp": 1 - t}
+        )
+
+    def a_copy(i):
+        src = abuf.at[pl.ds(pl.multiple_of(i * tok, tok), tok)]
+        dst = abuf.at[pl.ds(pl.multiple_of(rows_own + i * tok, tok), tok)]
+        return remote(src, dst, a_send.at[i], a_recv.at[i], {"seq": z + inward})
+
+    def c_copy(s, j):
+        at = lax.rem(s, owned)
+        return remote(
+            csend.at[at, j], cbuf.at[at, j], c_send.at[at, j], c_recv.at[at, j],
+            {"seq": z - inward},
+        )
+
+    def kv_copy(s, way, own):
+        dst = kvbuf.at[pl.ds(first, spans), :, :, s]
+        to = z - 1 if way == 0 else z + 1
+        return remote(kv_ref if own else dst, dst, kv_send.at[way, s], kv_recv.at[s], {"seq": to})
+
+    def kv_core(s):
+        part = kvbuf.at[pl.ds(0, spans), :, :, s]
+        return remote(part, part, kvc_send.at[s], kvc_recv.at[s], {"span": 1 - c})
 
     def local_w(j):
-        return pltpu.make_async_copy(
-            w_ref.at[:, pl.ds(pl.multiple_of(j * sub, sub), sub)], wbuf.at[z, j], loc.at[j]
-        )
+        return pltpu.make_async_copy(w_ref.at[:, columns(j)], wbuf.at[z, j], loc.at[j])
 
     def local_kv():
         return pltpu.make_async_copy(
             kv_ref, kvbuf.at[pl.ds(first, spans), :, :, z], loc.at[parts]
         )
 
+    reach = ((0, z > 0), (1, z < last))
+
     barrier = pltpu.get_barrier_semaphore()
-    for peer in range(n):
-        @pl.when(z != peer)
-        def _(peer=peer):
-            pl.semaphore_signal(barrier, inc=1, device_id={"seq": peer}, device_id_type=MESH)
+    for way, ok in reach:
+        @pl.when(ok)
+        def _(way=way):
+            to = z - 1 if way == 0 else z + 1
+            pl.semaphore_signal(barrier, inc=1, device_id={"seq": to}, device_id_type=MESH)
     pl.semaphore_signal(barrier, inc=1, device_id={"rep": 1 - y}, device_id_type=MESH)
     pl.semaphore_signal(barrier, inc=1, device_id={"span": 1 - c}, device_id_type=MESH)
     pl.semaphore_signal(barrier, inc=1, device_id={"tp": 1 - t}, device_id_type=MESH)
-    pl.semaphore_wait(barrier, n - 1 + 3)
-
+    pl.semaphore_wait(barrier, jnp.where(is_end, 4, 5))
+
+    for way, ok in reach:
+        @pl.when(ok)
+        def _(way=way):
+            kv_copy(z, way, True).start()
     local_kv().start()
-    for peer in range(n):
-        @pl.when(z != peer)
-        def _(peer=peer):
-            kv_copy(peer, z).start()
-    for j in range(parts):
-        @pl.when(z > 0)
-        def _(j=j):
-            z_copy(z, j, 0, True).start()
-
-        @pl.when(z < n - 1)
-        def _(j=j):
-            z_copy(z, j, 1, True).start()
-    for j in range(parts):
-        local_w(j).start()
-
-    local_kv().wait()
-    for peer in range(n):
-        @pl.when(z != peer)
-        def _(peer=peer):
-            kv_copy(peer, peer).wait_recv()
-
-    @pl.when(c == 0)
-    def _():
-        kv_core().start()
+    for way, ok in reach:
+        @pl.when(ok)
+        def _(way=way):
+            z_copy(z, 0, way, True).start()
+
+    def own_weights(way, ok):
+        @pl.when(ok)
+        def _():
+            for j in range(1, parts):
+                z_copy(z, j, way, True).start()
+
+    for d in range(n):
+        if d == 0:
+            local_kv().wait()
+
+            @pl.when(c == 0)
+            def _():
+                kv_core(z).start()
+        else:
+            for sign in (-1, 1):
+                s = z + sign * d
+
+                @pl.when(both(s >= 0, s < n))
+                def _(s=s, sign=sign):
+                    way = 0 if sign > 0 else 1
+                    kv_copy(s, way, False).wait_recv()
+
+                    @pl.when(reach[way][1])
+                    def _():
+                        kv_copy(s, way, False).start()
+
+                    @pl.when(c == 0)
+                    def _():
+                        kv_core(s).start()
+        own_weights(0, both(z > 0, last - z == d))
+        own_weights(1, both(z < last, z == d))
+        if d == 0:
+            for j in range(parts):
+                local_w(j).start()
 
     @pl.when(c != 0)
     def _():
-        kv_core().wait_recv()
+        for s in range(n):
+            kv_core(s).wait_recv()
 
     def each(e, low, do):
-        ok = jnp.logical_and(e >= low, e < steps)
+        ok = both(e >= low, e < steps)
         d, j = e // parts + 1, e % parts
         for sign in (-1, 1):
             s = z + sign * d
 
-            @pl.when(jnp.logical_and(ok, jnp.logical_and(s >= 0, s < n)))
+            @pl.when(both(ok, both(s >= 0, s < n)))
             def _(s=s, sign=sign):
                 do(s, j, sign)
 
     def arrive(s, j, sign):
         way = 0 if sign > 0 else 1
-        z_copy(s, j, way, False).wait_recv()
-
-        @pl.when((z > 0) if way == 0 else (z < n - 1))
-        def _():
-            z_copy(s, j, way, False).start()
-
-        y_copy(s, j).start()
-        core_copy(s, j, 0).start()
+
+        @pl.when(wanted(z, s, j))
+        def _():
+            z_copy(s, j, way, False).wait_recv()
+
+            @pl.when(both(reach[way][1], wanted(z - sign, s, j)))
+            def _():
+                z_copy(s, j, way, False).start()
+
+            @pl.when(jnp.logical_not(whole(s, j)))
+            def _():
+                y_copy(s, j).start()
+
+            core_copy(s, j, 0).start()
 
     def pass_on(s, j, sign):
-        y_copy(s, j).wait_recv()
-        core_copy(s, j, 1).start()
+        @pl.when(both(wanted(z, s, j), jnp.logical_not(whole(s, j))))
+        def _():
+            y_copy(s, j).wait_recv()
+            core_copy(s, j, 1).start()
 
     def project(s, j):
-        part = jnp.dot(abuf[...], wbuf[s, j], preferred_element_type=jnp.float32)
+        part = jnp.dot(
+            abuf[pl.ds(0, rows_own)], wbuf[s, j], preferred_element_type=jnp.float32
+        )
         at = lax.rem(s, owned)
 
         @pl.when(s // owned == t)
@@ -154,28 +223,63 @@
         @pl.when(s // owned != t)
         def _():
             xsend[at, j] = part.astype(jnp.bfloat16)
-            x_copy(s, j).start()
-
-    def gather_project(s, j, sign):
+            x_copy(s, j, xsend).start()
+
+    def project_guest(s, j):
+        part = jnp.dot(
+            abuf[pl.ds(rows_own, rows_own)], wbuf[s, j], preferred_element_type=jnp.float32
+        )
+        csend[lax.rem(s, owned), j] = part.astype(jnp.bfloat16)
+        c_copy(s, j).start()
+
+    def gathered(s, j):
         core_copy(s, j, 0).wait_recv()
         core_copy(s, j, 1).wait_recv()
         project(s, j)
 
-    def finish(s, j, sign):
+    def gather_project(s, j, sign):
+        @pl.when(both(wanted(z, s, j), jnp.logical_not(whole(s, j))))
+        def _():
+            gathered(s, j)
+
+        @pl.when(jnp.logical_not(wanted(z, s, j)))
+        def _():
+            c_copy(s, j).wait_recv()
+
+            @pl.when(s // owned != t)
+            def _():
+                x_copy(s, j, cbuf).start()
+
+    def finish(s, j):
         @pl.when(s // owned == t)
         def _():
-            x_copy(s, j).wait_recv()
+            x_copy(s, j, xsend).wait_recv()
             at = lax.rem(s, owned)
             where = pl.ds(pl.multiple_of(at * cols + j * sub, 128), sub)
-            for i in range(spans):
-                level = plan_ref[first + i]
-                gate = noise_ref[pl.ds(level, 1), where]
-                mine = pl.ds(i * tok, tok)
-                total = pbuf[at, j, mine, :] + xbuf[at, j, mine, :].astype(jnp.float32)
-                out_ref[mine, where] = (total * gate).astype(out_ref.dtype)
+
+            def put(mine):
+                for i in range(spans):
+                    level = plan_ref[first + i]
+                    gate = noise_ref[pl.ds(level, 1), where]
+                    span = pl.ds(i * tok, tok)
+                    total = mine(at, span) + xbuf[at, j, span, :].astype(jnp.float32)
+                    out_ref[span, where] = (total * gate).astype(out_ref.dtype)
+
+            @pl.when(wanted(z, s, j))
+            def _():
+                put(lambda at, span: pbuf[at, j, span, :])
+
+            @pl.when(jnp.logical_not(wanted(z, s, j)))
+            def _():
+                put(lambda at, span: cbuf[at, j, span, :].astype(jnp.float32))
+
+    def finish_in_line(s, j, sign):
+        @pl.when(jnp.logical_not(whole(s, j)))
+        def _():
+            finish(s, j)
 
     units = spans * kvh
-    lag = units - 1
+    lag = 2
     lead = per_kv * tok
 
     def attend(u, carry):
@@ -210,11 +314,21 @@
                 pl.ds(pl.multiple_of(i * tok, tok), tok),
                 pl.ds(pl.multiple_of((g * per_kv + h) * hd, hd), hd),
             ] = result[h]
+
+        @pl.when(both(is_end, g == kvh - 1))
+        def _():
+            a_copy(i).start()
+
         each(u, 0, arrive)
         each(u - lag, 0, pass_on)
         return carry
 
     lax.fori_loop(0, units, attend, 0)
+
+    @pl.when(is_end)
+    def _():
+        for j in range(late, parts):
+            rest_copy(z, j).start()
 
     def own(j, carry):
         local_w(j).wait()
@@ -223,45 +337,105 @@
 
     lax.fori_loop(0, parts, own, 0)
 
+    turn = jnp.where(c == 0, 6, 7)
+    due = 12
+    own_done = 10
+
     def run(e, carry):
         each(e, units, arrive)
         each(e - lag, units - lag, pass_on)
+
+        @pl.when(both(is_host, e == turn))
+        def _():
+            for i in range(spans):
+                a_copy(i).wait_recv()
+
+            def catch_up(f, carry):
+                project_guest(z + inward * (f // parts + 1), f % parts)
+                return carry
+
+            lax.fori_loop(keep - parts, turn - lag - 1, catch_up, 0)
+
         each(e - lag - 1, 0, gather_project)
-        each(e - lag - 3, 0, finish)
+        f = e - lag - 1
+        s = z + inward * (f // parts + 1)
+        inside = both(f >= keep - parts, f < (n - 2) * parts)
+
+        @pl.when(both(both(is_host, e >= turn), inside))
+        def _():
+            project_guest(s, f % parts)
+
+        k = e - due + late
+
+        @pl.when(both(is_host, both(k >= late, k < parts)))
+        def _():
+            rest_copy(guest, k).wait_recv()
+            core_copy(guest, k, 1).start()
+
+        @pl.when(both(is_host, both(k - 1 >= late, k - 1 < parts)))
+        def _():
+            gathered(guest, k - 1)
+
+        each(e - lag - 3, 0, finish_in_line)
+
+        @pl.when(both(is_host, both(k - 3 >= late, k - 3 < parts)))
+        def _():
+            finish(guest, k - 3)
+
+        m = e - own_done
+
+        @pl.when(both(m >= 0, m < parts))
+        def _():
+            finish(z, m)
+
         return carry
 
-    lax.fori_loop(0, parts, lambda j, carry: (finish(z, j, 0), carry)[1], 0)
-    lax.fori_loop(units, max(steps, units) + lag + 3, run, 0)
-
-    for peer in range(n):
-        @pl.when(z != peer)
-        def _(peer=peer):
-            kv_copy(peer, z).wait_send()
-
-    @pl.when(c == 0)
+    lax.fori_loop(lag + 1, max(steps + lag + 3, due + parts - late + 3, own_done + parts), run, 0)
+
+    for s in range(n):
+        for way, ok in reach:
+            @pl.when(both(ok, (z <= s) if way == 0 else (z >= s)))
+            def _(s=s, way=way):
+                kv_copy(s, way, False).wait_send()
+
+        @pl.when(c == 0)
+        def _(s=s):
+            kv_core(s).wait_send()
+
+    @pl.when(is_end)
     def _():
-        kv_core().wait_send()
+        for i in range(spans):
+            a_copy(i).wait_send()
+        for j in range(late, parts):
+            rest_copy(z, j).wait_send()
 
     def drain(f, carry):
         s, j = f // parts, f % parts
 
-        @pl.when(jnp.logical_and(z > 0, s >= z))
+        @pl.when(both(both(z > 0, s >= z), wanted(z - 1, s, j)))
         def _():
             z_copy(s, j, 0, False).wait_send()
 
-        @pl.when(jnp.logical_and(z < n - 1, s <= z))
+        @pl.when(both(both(z < last, s <= z), wanted(z + 1, s, j)))
         def _():
             z_copy(s, j, 1, False).wait_send()
 
-        @pl.when(s != z)
+        @pl.when(both(s != z, wanted(z, s, j)))
         def _():
             core_copy(s, j, 0).wait_send()
             core_copy(s, j, 1).wait_send()
-            y_copy(s, j).wait_send()
+
+            @pl.when(jnp.logical_not(whole(s, j)))
+            def _():
+                y_copy(s, j).wait_send()
 
         @pl.when(s // owned != t)
         def _():
-            x_copy(s, j).wait_send()
+            x_copy(s, j, xsend).wait_send()
+
+        @pl.when(both(is_host, both(s != z, jnp.logical_not(wanted(guest, s, j)))))
+        def _():
+            c_copy(s, j).wait_send()
 
         return carry
 
@@ -274,12 +448,14 @@
     depth, cols = out_weight.shape
     n, tps, cores = lax.axis_size("seq"), lax.axis_size("tp"), lax.axis_size("span")
     sub, owned, wide = cols // parts, n // tps, noise_table.shape[1]
+    keep, late = parts, parts // 3
     q = jnp.transpose(queries, (0, 2, 1, 3))
     kv = jnp.stack([key_states, value_states], axis=0).transpose(1, 3, 0, 2, 4)
     vmem = pl.BlockSpec(memory_space=pltpu.VMEM)
     dma = pltpu.SemaphoreType.DMA
+    tile = (owned, parts, spans * tok, sub)
     out = pl.pallas_call(
-        functools.partial(fused_kernel, parts),
+        functools.partial(fused_kernel, parts, keep, late),
         out_shape=jax.ShapeDtypeStruct((spans * tok, wide), jnp.bfloat16),
         in_specs=[
             pl.BlockSpec(memory_space=pltpu.SMEM), vmem, vmem, vmem,
@@ -289,13 +465,16 @@
         scratch_shapes=[
             pltpu.VMEM((spans * cores, kvh, 2, n, tok, hd), jnp.bfloat16),
             pltpu.VMEM((n, parts, depth, sub), jnp.bfloat16),
-            pltpu.VMEM((spans * tok, depth), jnp.bfloat16),
-            pltpu.VMEM((owned, parts, spans * tok, sub), jnp.float32),
-            pltpu.VMEM((owned, parts, spans * tok, sub), jnp.bfloat16),
-            pltpu.VMEM((owned, parts, spans * tok, sub), jnp.bfloat16),
-            dma((n,)), dma((n,)), dma((2,)), dma((parts + 1,)),
-            dma((2, n, parts)), dma((2, n, parts)), dma((n, parts)),
-            dma((n, parts)), dma((2, n, parts)), dma((n, parts)),
+            pltpu.VMEM((2 * spans * tok, depth), jnp.bfloat16),
+            pltpu.VMEM(tile, jnp.float32),
+            pltpu.VMEM(tile, jnp.bfloat16),
+            pltpu.VMEM(tile, jnp.bfloat16),
+            pltpu.VMEM(tile, jnp.bfloat16),
+            pltpu.VMEM(tile, jnp.bfloat16),
+            dma((2, n)), dma((n,)), dma((n,)), dma((n,)), dma((parts + 1,)),
+            dma((2, n, parts)), dma((n, parts)), dma((parts,)), dma((parts,)),
+            dma((2, n, parts)), dma((2, n, parts)), dma((n, parts)), dma((n, parts)),
+            dma((owned, parts)), dma((owned, parts)), dma((spans,)), dma((spans,)),
             dma((owned, parts)), dma((owned, parts)),
         ],
         compiler_params=pltpu.CompilerParams(
@@ -398,7 +577,8 @@
     parts = choose_parts(cols)
     pairs = all(lax.axis_size(name) == 2 for name in ("rep", "span", "tp"))
     args = (queries, key_states, value_states, out_weight, noise_table, plan)
-    if pairs and parts and depth % (copies * 16) == 0 and lax.axis_size("seq") % 2 == 0:
+    line = lax.axis_size("seq") == 2 * lax.axis_size("tp")
+    if pairs and parts and depth % (copies * 16) == 0 and line:
         return fused(parts, *args)
     return per_device(*args)
 

time: 137 us -> 120 us (0.88)
  Pallas kernels: 132 us -> 115 us
    pallas_call x1, Pallas kernels: 132 us -> 115 us  [fused(): pl.pallas_call(functools.partial(fused_kernel, parts, keep, late), out_sh...]
where the time goes in v1:
time: 120 us; the launch traced here: 119 us
  Pallas kernels  115 us (96%)
  local copies, waits for them, and re-layouts  3.65 us (3%)
    pallas_call x1, Pallas kernels, fused(): pl.pallas_call(functools.partial(fused_kernel, parts, keep, late), out_sh...  115 us
    unnamed x1, local copies, waits for them, and re-layouts  2.65 us

profile of v1, /device:TPU:2, one launch (start us, length us, event | category | flops | bytes accessed | tf_op | source)
XLA Modules:
  0.0 119.0 jit_solution(18380715169581850811)
XLA Ops:
  0.0 1.0 copy_bitcast_fusion
  1.0 0.7 maximum_bitcast_fusion.kv_ref
  1.7 114.6 %relay_attention.1 = bf16[256,3072]{1,0:T(8,128)(2,1)} custom-call(s32[4]{0:T(128)} %plan_ref.1, bf16[2,12,128,128]{3,2,1,0:T(8,128)(2,1)} %bitcast.9, bf16[2,2,2,128,128]{4,3,2,1,0:T(8,128)(2,1)} %maximum_bitcast_fusion.kv_ref, f32[64,3072]{1,0:T(8,128)} %noise_ref.1, bf16[1536,1536]{1,0:T(8,128)(2,1)} %w_ref.1), custom_call_target="tpu_custom_call" | custom-call | tf_op jit(solution)/shard_map/relay_attention/pallas_call | solution.py:457
  116.4 2.7 %copy.12 = bf16[2,128,3072]{2,1,0:T(8,128)(2,1)} copy(bf16[2,128,3072]{2,1,0:T(8,128)(2,1)} %bitcast.8) | data formatting | bytes 3145728

commit v2 on v1

--- a/solution.py
+++ b/solution.py
@@ -12,7 +12,7 @@
 
 
 def fused_kernel(
-    parts, keep, late, plan_ref, q_ref, kv_ref, noise_ref, w_ref, out_ref,
+    parts, keep, late, ahead, plan_ref, q_ref, kv_ref, noise_ref, w_ref, out_ref,
     kvbuf, wbuf, abuf, pbuf, xsend, xbuf, csend, cbuf,
     kv_send, kv_recv, kvc_send, kvc_recv, loc, wz_send, wz_recv, wf_send, wf_recv,
     wc_send, wc_recv, wy_send, wy_recv, x_send, x_recv, a_send, a_recv, c_send, c_recv,
@@ -40,8 +40,11 @@
     is_host = jnp.logical_or(z == 1, z == n - 2)
     guest = z - inward
 
+    def place(r, s, j):
+        return (jnp.abs(s - r) - 1) * parts + j - keep
+
     def wanted(r, s, j):
-        far = (jnp.abs(s - r) - 1) * parts + j >= keep
+        far = place(r, s, j) >= 0
         return jnp.logical_not(both(jnp.logical_or(r == 0, r == last), far))
 
     def whole(s, j):
@@ -62,7 +65,7 @@
     def z_copy(s, j, way, own):
         dst = wbuf.at[s, j, rows(y, c)]
         src = w_ref.at[rows(y, c), columns(j)] if own else dst
-        to = z - 1 if way == 0 else z + 1
+        to = z + 2 * way - 1
         return remote(src, dst, wz_send.at[way, s, j], wz_recv.at[s, j], {"seq": to})
 
     def rest_copy(s, j):
@@ -82,7 +85,7 @@
     def x_copy(s, j, src):
         at = lax.rem(s, owned)
         return remote(
-            src.at[at, j], xbuf.at[at, j], x_send.at[at, j], x_recv.at[at, j], {"tp": 1 - t}
+            src, xbuf.at[at, j], x_send.at[at, j], x_recv.at[at, j], {"tp": 1 - t}
         )
 
     def a_copy(i):
@@ -90,21 +93,20 @@
         dst = abuf.at[pl.ds(pl.multiple_of(rows_own + i * tok, tok), tok)]
         return remote(src, dst, a_send.at[i], a_recv.at[i], {"seq": z + inward})
 
-    def c_copy(s, j):
-        at = lax.rem(s, owned)
+    def c_copy(f):
         return remote(
-            csend.at[at, j], cbuf.at[at, j], c_send.at[at, j], c_recv.at[at, j],
-            {"seq": z - inward},
-        )
-
-    def kv_copy(s, way, own):
-        dst = kvbuf.at[pl.ds(first, spans), :, :, s]
+            csend.at[f], cbuf.at[f], c_send.at[f], c_recv.at[f], {"seq": z - inward}
+        )
+
+    def kv_copy(s, g, way, own):
+        dst = kvbuf.at[pl.ds(first, spans), g, :, s]
+        src = kv_ref.at[:, g] if own else dst
         to = z - 1 if way == 0 else z + 1
-        return remote(kv_ref if own else dst, dst, kv_send.at[way, s], kv_recv.at[s], {"seq": to})
-
-    def kv_core(s):
-        part = kvbuf.at[pl.ds(0, spans), :, :, s]
-        return remote(part, part, kvc_send.at[s], kvc_recv.at[s], {"span": 1 - c})
+        return remote(src, dst, kv_send.at[way, s, g], kv_recv.at[s, g], {"seq": to})
+
+    def kv_core(s, g):
+        part = kvbuf.at[pl.ds(0, spans), g, :, s]
+        return remote(part, part, kvc_send.at[s, g], kvc_recv.at[s, g], {"span": 1 - c})
 
     def local_w(j):
         return pltpu.make_async_copy(w_ref.at[:, columns(j)], wbuf.at[z, j], loc.at[j])
@@ -127,55 +129,59 @@
     pl.semaphore_signal(barrier, inc=1, device_id={"tp": 1 - t}, device_id_type=MESH)
     pl.semaphore_wait(barrier, jnp.where(is_end, 4, 5))
 
-    for way, ok in reach:
-        @pl.when(ok)
-        def _(way=way):
-            kv_copy(z, way, True).start()
+    for g in range(kvh):
+        for way, ok in reach:
+            @pl.when(ok)
+            def _(g=g, way=way):
+                kv_copy(z, g, way, True).start()
     local_kv().start()
-    for way, ok in reach:
-        @pl.when(ok)
-        def _(way=way):
-            z_copy(z, 0, way, True).start()
-
-    def own_weights(way, ok):
-        @pl.when(ok)
-        def _():
-            for j in range(1, parts):
+
+    def own_weights(way, low, high, ok):
+        for j in range(low, high):
+            @pl.when(both(ok, wanted(z + 2 * way - 1, z, j)))
+            def _(j=j):
                 z_copy(z, j, way, True).start()
 
     for d in range(n):
-        if d == 0:
-            local_kv().wait()
-
-            @pl.when(c == 0)
-            def _():
-                kv_core(z).start()
-        else:
+        for g in range(kvh):
+            if d == 0:
+                if g == 0:
+                    local_kv().wait()
+
+                @pl.when(c == 0)
+                def _(g=g):
+                    kv_core(z, g).start()
+
+                continue
             for sign in (-1, 1):
                 s = z + sign * d
 
                 @pl.when(both(s >= 0, s < n))
-                def _(s=s, sign=sign):
+                def _(s=s, sign=sign, g=g):
                     way = 0 if sign > 0 else 1
-                    kv_copy(s, way, False).wait_recv()
+                    kv_copy(s, g, way, False).wait_recv()
 
                     @pl.when(reach[way][1])
                     def _():
-                        kv_copy(s, way, False).start()
+                        kv_copy(s, g, way, False).start()
 
                     @pl.when(c == 0)
                     def _():
-                        kv_core(s).start()
-        own_weights(0, both(z > 0, last - z == d))
-        own_weights(1, both(z < last, z == d))
+                        kv_core(s, g).start()
         if d == 0:
+            own_weights(0, 0, ahead, z == last)
+            own_weights(1, 0, ahead, z == 0)
             for j in range(parts):
                 local_w(j).start()
+        else:
+            own_weights(0, 0, parts, both(z > 0, last - z == d))
+            own_weights(1, 0, parts, both(z < last, z == d))
 
     @pl.when(c != 0)
     def _():
         for s in range(n):
-            kv_core(s).wait_recv()
+            for g in range(kvh):
+                kv_core(s, g).wait_recv()
 
     def each(e, low, do):
         ok = both(e >= low, e < steps)
@@ -188,13 +194,14 @@
                 do(s, j, sign)
 
     def arrive(s, j, sign):
-        way = 0 if sign > 0 else 1
+        way = (1 - sign) // 2
+        onward = z - sign
 
         @pl.when(wanted(z, s, j))
         def _():
             z_copy(s, j, way, False).wait_recv()
 
-            @pl.when(both(reach[way][1], wanted(z - sign, s, j)))
+            @pl.when(both(both(onward >= 0, onward < n), wanted(onward, s, j)))
             def _():
                 z_copy(s, j, way, False).start()
 
@@ -204,6 +211,11 @@
 
             core_copy(s, j, 0).start()
 
+    def arrive_in_line(s, j, sign):
+        @pl.when(jnp.logical_not(both(is_host, both(s == guest, j >= ahead))))
+        def _():
+            arrive(s, j, sign)
+
     def pass_on(s, j, sign):
         @pl.when(both(wanted(z, s, j), jnp.logical_not(whole(s, j))))
         def _():
@@ -223,14 +235,15 @@
         @pl.when(s // owned != t)
         def _():
             xsend[at, j] = part.astype(jnp.bfloat16)
-            x_copy(s, j, xsend).start()
+            x_copy(s, j, xsend.at[at, j]).start()
 
     def project_guest(s, j):
         part = jnp.dot(
             abuf[pl.ds(rows_own, rows_own)], wbuf[s, j], preferred_element_type=jnp.float32
         )
-        csend[lax.rem(s, owned), j] = part.astype(jnp.bfloat16)
-        c_copy(s, j).start()
+        f = place(guest, s, j)
+        csend[f] = part.astype(jnp.bfloat16)
+        c_copy(f).start()
 
     def gathered(s, j):
         core_copy(s, j, 0).wait_recv()
@@ -244,39 +257,39 @@
 
         @pl.when(jnp.logical_not(wanted(z, s, j)))
         def _():
-            c_copy(s, j).wait_recv()
+            f = place(z, s, j)
+            c_copy(f).wait_recv()
 
             @pl.when(s // owned != t)
             def _():
-                x_copy(s, j, cbuf).start()
-
-    def finish(s, j):
-        @pl.when(s // owned == t)
-        def _():
-            x_copy(s, j, xsend).wait_recv()
-            at = lax.rem(s, owned)
-            where = pl.ds(pl.multiple_of(at * cols + j * sub, 128), sub)
-
-            def put(mine):
-                for i in range(spans):
-                    level = plan_ref[first + i]
-                    gate = noise_ref[pl.ds(level, 1), where]
-                    span = pl.ds(i * tok, tok)
-                    total = mine(at, span) + xbuf[at, j, span, :].astype(jnp.float32)
-                    out_ref[span, where] = (total * gate).astype(out_ref.dtype)
-
-            @pl.when(wanted(z, s, j))
-            def _():
-                put(lambda at, span: pbuf[at, j, span, :])
-
-            @pl.when(jnp.logical_not(wanted(z, s, j)))
-            def _():
-                put(lambda at, span: cbuf[at, j, span, :].astype(jnp.float32))
-
-    def finish_in_line(s, j, sign):
-        @pl.when(jnp.logical_not(whole(s, j)))
-        def _():
-            finish(s, j)
+                x_copy(s, j, cbuf.at[f]).start()
+
+    mine = t * owned
+    near = z // owned == t
+    front = jnp.where(near, z, jnp.where(inward > 0, mine, mine + owned - 1))
+    rear = 2 * mine + owned - 1 - front
+
+    def finish(q):
+        s, j = jnp.where(q < parts, front, rear), lax.rem(q, parts)
+        at = lax.rem(s, owned)
+        x_copy(s, j, xsend.at[at, j]).wait_recv()
+        where = pl.ds(pl.multiple_of(at * cols + j * sub, 128), sub)
+
+        def put(own):
+            for i in range(spans):
+                level = plan_ref[first + i]
+                gate = noise_ref[pl.ds(level, 1), where]
+                span = pl.ds(i * tok, tok)
+                total = own(span) + xbuf[at, j, span, :].astype(jnp.float32)
+                out_ref[span, where] = (total * gate).astype(out_ref.dtype)
+
+        @pl.when(wanted(z, s, j))
+        def _():
+            put(lambda span: pbuf[at, j, span, :])
+
+        @pl.when(jnp.logical_not(wanted(z, s, j)))
+        def _():
+            put(lambda span: cbuf[place(z, s, j), span, :].astype(jnp.float32))
 
     units = spans * kvh
     lag = 2
@@ -319,11 +332,13 @@
         def _():
             a_copy(i).start()
 
-        each(u, 0, arrive)
-        each(u - lag, 0, pass_on)
+        each(u, 0, arrive_in_line)
         return carry
 
     lax.fori_loop(0, units, attend, 0)
+
+    own_weights(0, ahead, parts, z == last)
+    own_weights(1, ahead, parts, z == 0)
 
     @pl.when(is_end)
     def _():
@@ -337,13 +352,18 @@
 
     lax.fori_loop(0, parts, own, 0)
 
-    turn = jnp.where(c == 0, 6, 7)
-    due = 12
-    own_done = 10
+    turn = jnp.where(c == 0, 4, 6)
+    shift, due, sums = 4, 2 * parts, 2 * parts
 
     def run(e, carry):
-        each(e, units, arrive)
-        each(e - lag, units - lag, pass_on)
+        each(e, units, arrive_in_line)
+        k = e - shift
+
+        @pl.when(both(is_host, both(k >= ahead, k < parts)))
+        def _():
+            arrive(guest, k, -inward)
+
+        each(e - lag, 0, pass_on)
 
         @pl.when(both(is_host, e == turn))
         def _():
@@ -351,19 +371,17 @@
                 a_copy(i).wait_recv()
 
             def catch_up(f, carry):
-                project_guest(z + inward * (f // parts + 1), f % parts)
+                project_guest(z + inward * (f // parts), f % parts)
                 return carry
 
-            lax.fori_loop(keep - parts, turn - lag - 1, catch_up, 0)
+            lax.fori_loop(keep, turn - lag - 1 + parts, catch_up, 0)
 
         each(e - lag - 1, 0, gather_project)
-        f = e - lag - 1
-        s = z + inward * (f // parts + 1)
-        inside = both(f >= keep - parts, f < (n - 2) * parts)
-
-        @pl.when(both(both(is_host, e >= turn), inside))
-        def _():
-            project_guest(s, f % parts)
+        f = e - lag - 1 + parts
+
+        @pl.when(both(both(is_host, e >= turn), f < (n - 1) * parts))
+        def _():
+            project_guest(z + inward * (f // parts), f % parts)
 
         k = e - due + late
 
@@ -376,31 +394,27 @@
         def _():
             gathered(guest, k - 1)
 
-        each(e - lag - 3, 0, finish_in_line)
-
-        @pl.when(both(is_host, both(k - 3 >= late, k - 3 < parts)))
-        def _():
-            finish(guest, k - 3)
-
-        m = e - own_done
-
-        @pl.when(both(m >= 0, m < parts))
-        def _():
-            finish(z, m)
+        q = e - sums
+
+        @pl.when(both(q >= 0, q < owned * parts))
+        def _():
+            finish(q)
 
         return carry
 
-    lax.fori_loop(lag + 1, max(steps + lag + 3, due + parts - late + 3, own_done + parts), run, 0)
+    lax.fori_loop(lag, max(steps + lag + 1, due + parts - late + 1, sums + owned * parts), run, 0)
 
     for s in range(n):
         for way, ok in reach:
             @pl.when(both(ok, (z <= s) if way == 0 else (z >= s)))
             def _(s=s, way=way):
-                kv_copy(s, way, False).wait_send()
+                for g in range(kvh):
+                    kv_copy(s, g, way, False).wait_send()
 
         @pl.when(c == 0)
         def _(s=s):
-            kv_core(s).wait_send()
+            for g in range(kvh):
+                kv_core(s, g).wait_send()
 
     @pl.when(is_end)
     def _():
@@ -431,11 +445,11 @@
 
         @pl.when(s // owned != t)
         def _():
-            x_copy(s, j, xsend).wait_send()
-
-        @pl.when(both(is_host, both(s != z, jnp.logical_not(wanted(guest, s, j)))))
-        def _():
-            c_copy(s, j).wait_send()
+            x_copy(s, j, xsend.at[lax.rem(s, owned), j]).wait_send()
+
+        @pl.when(both(is_host, jnp.logical_not(wanted(guest, s, j))))
+        def _():
+            c_copy(place(guest, s, j)).wait_send()
 
         return carry
 
@@ -448,14 +462,15 @@
     depth, cols = out_weight.shape
     n, tps, cores = lax.axis_size("seq"), lax.axis_size("tp"), lax.axis_size("span")
     sub, owned, wide = cols // parts, n // tps, noise_table.shape[1]
-    keep, late = parts, parts // 3
+    keep, late, ahead = parts // 2, parts // 3, parts - parts // 3
+    extra = (n - 1) * parts - keep
     q = jnp.transpose(queries, (0, 2, 1, 3))
     kv = jnp.stack([key_states, value_states], axis=0).transpose(1, 3, 0, 2, 4)
     vmem = pl.BlockSpec(memory_space=pltpu.VMEM)
     dma = pltpu.SemaphoreType.DMA
     tile = (owned, parts, spans * tok, sub)
     out = pl.pallas_call(
-        functools.partial(fused_kernel, parts, keep, late),
+        functools.partial(fused_kernel, parts, keep, late, ahead),
         out_shape=jax.ShapeDtypeStruct((spans * tok, wide), jnp.bfloat16),
         in_specs=[
             pl.BlockSpec(memory_space=pltpu.SMEM), vmem, vmem, vmem,
@@ -469,13 +484,13 @@
             pltpu.VMEM(tile, jnp.float32),
             pltpu.VMEM(tile, jnp.bfloat16),
             pltpu.VMEM(tile, jnp.bfloat16),
-            pltpu.VMEM(tile, jnp.bfloat16),
-            pltpu.VMEM(tile, jnp.bfloat16),
-            dma((2, n)), dma((n,)), dma((n,)), dma((n,)), dma((parts + 1,)),
+            pltpu.VMEM((extra, spans * tok, sub), jnp.bfloat16),
+            pltpu.VMEM((extra, spans * tok, sub), jnp.bfloat16),
+            dma((2, n, kvh)), dma((n, kvh)), dma((n, kvh)), dma((n, kvh)), dma((parts + 1,)),
             dma((2, n, parts)), dma((n, parts)), dma((parts,)), dma((parts,)),
             dma((2, n, parts)), dma((2, n, parts)), dma((n, parts)), dma((n, parts)),
             dma((owned, parts)), dma((owned, parts)), dma((spans,)), dma((spans,)),
-            dma((owned, parts)), dma((owned, parts)),
+            dma((extra,)), dma((extra,)),
         ],
         compiler_params=pltpu.CompilerParams(
             collective_id=0, has_side_effects=True, vmem_limit_bytes=60 * 1024 * 1024

time: 120 us -> 107 us (0.89)
  Pallas kernels: 115 us -> 101 us
    pallas_call x1, Pallas kernels: 115 us -> 101 us  [fused(): pl.pallas_call(functools.partial(fused_kernel, parts, keep, late, ahead),...]
where the time goes in v2:
time: 107 us; the launch traced here: 106 us
  Pallas kernels  101 us (94%)
  local copies, waits for them, and re-layouts  3.65 us (3%)
    pallas_call x1, Pallas kernels, fused(): pl.pallas_call(functools.partial(fused_kernel, parts, keep, late, ahead),...  101 us
    unnamed x1, local copies, waits for them, and re-layouts  2.65 us

profile of v2, /device:TPU:2, one launch (start us, length us, event | category | flops | bytes accessed | tf_op | source)
XLA Modules:
  0.0 105.6 jit_solution(14238636858285723795)
XLA Ops:
  0.0 1.0 copy_bitcast_fusion
  1.0 0.7 maximum_bitcast_fusion.kv_ref
  1.7 101.2 %relay_attention.1 = bf16[256,3072]{1,0:T(8,128)(2,1)} custom-call(s32[4]{0:T(128)} %plan_ref.1, bf16[2,12,128,128]{3,2,1,0:T(8,128)(2,1)} %bitcast.9, bf16[2,2,2,128,128]{4,3,2,1,0:T(8,128)(2,1)} %maximum_bitcast_fusion.kv_ref, f32[64,3072]{1,0:T(8,128)} %noise_ref.1, bf16[1536,1536]{1,0:T(8,128)(2,1)} %w_ref.1), custom_call_target="tpu_custom_call" | custom-call | tf_op jit(solution)/shard_map/relay_attention/pallas_call | solution.py:472
  102.9 2.7 %copy.12 = bf16[2,128,3072]{2,1,0:T(8,128)(2,1)} copy(bf16[2,128,3072]{2,1,0:T(8,128)(2,1)} %bitcast.8) | data formatting | bytes 3145728

commit v3 on v2

--- a/solution.py
+++ b/solution.py
@@ -22,7 +22,7 @@
     n = lax.axis_size("seq")
     cores, tps = lax.axis_size("span"), lax.axis_size("tp")
     spans, heads, tok, hd = q_ref.shape
-    kvh = kv_ref.shape[1]
+    kvh = kv_ref.shape[0]
     per_kv = heads // kvh
     depth, cols = w_ref.shape
     quarter = depth // (cores * lax.axis_size("rep"))
@@ -31,14 +31,19 @@
     rows_own = spans * tok
     first = c * spans
     last = n - 1
-    steps = last * parts
     scale = hd ** (-0.5) * math.log2(math.e)
     both = jnp.logical_and
 
     is_end = jnp.logical_or(z == 0, z == last)
+    is_host = jnp.logical_not(is_end)
     inward = jnp.where(2 * z < n, 1, -1)
-    is_host = jnp.logical_or(z == 1, z == n - 2)
+    way_in = (1 + inward) // 2
+    way_out = 1 - way_in
     guest = z - inward
+    length = jnp.where(is_end, last, last - 1) * parts
+
+    def source(e):
+        return z + inward * (e // parts + 1), e % parts
 
     def place(r, s, j):
         return (jnp.abs(s - r) - 1) * parts + j - keep
@@ -99,13 +104,13 @@
         )
 
     def kv_copy(s, g, way, own):
-        dst = kvbuf.at[pl.ds(first, spans), g, :, s]
-        src = kv_ref.at[:, g] if own else dst
-        to = z - 1 if way == 0 else z + 1
+        dst = kvbuf.at[s, g, :, pl.ds(first, spans)]
+        src = kv_ref.at[g] if own else dst
+        to = z + 2 * way - 1
         return remote(src, dst, kv_send.at[way, s, g], kv_recv.at[s, g], {"seq": to})
 
     def kv_core(s, g):
-        part = kvbuf.at[pl.ds(0, spans), g, :, s]
+        part = kvbuf.at[s, g, :, pl.ds(0, spans)]
         return remote(part, part, kvc_send.at[s, g], kvc_recv.at[s, g], {"span": 1 - c})
 
     def local_w(j):
@@ -113,7 +118,7 @@
 
     def local_kv():
         return pltpu.make_async_copy(
-            kv_ref, kvbuf.at[pl.ds(first, spans), :, :, z], loc.at[parts]
+            kv_ref, kvbuf.at[z, :, :, pl.ds(first, spans)], loc.at[parts]
         )
 
     reach = ((0, z > 0), (1, z < last))
@@ -136,62 +141,35 @@
                 kv_copy(z, g, way, True).start()
     local_kv().start()
 
-    def own_weights(way, low, high, ok):
+    def own_weights(way, low, high):
         for j in range(low, high):
-            @pl.when(both(ok, wanted(z + 2 * way - 1, z, j)))
-            def _(j=j):
-                z_copy(z, j, way, True).start()
-
-    for d in range(n):
+            z_copy(z, j, way, True).start()
+
+    for j in range(parts):
+        local_w(j).start()
+
+    @pl.when(is_end)
+    def _():
+        own_weights(way_in, 0, ahead)
+
+    local_kv().wait()
+
+    @pl.when(c == 0)
+    def _():
         for g in range(kvh):
-            if d == 0:
-                if g == 0:
-                    local_kv().wait()
-
-                @pl.when(c == 0)
-                def _(g=g):
-                    kv_core(z, g).start()
-
-                continue
-            for sign in (-1, 1):
-                s = z + sign * d
-
-                @pl.when(both(s >= 0, s < n))
-                def _(s=s, sign=sign, g=g):
-                    way = 0 if sign > 0 else 1
-                    kv_copy(s, g, way, False).wait_recv()
-
-                    @pl.when(reach[way][1])
-                    def _():
-                        kv_copy(s, g, way, False).start()
-
-                    @pl.when(c == 0)
-                    def _():
-                        kv_core(s, g).start()
-        if d == 0:
-            own_weights(0, 0, ahead, z == last)
-            own_weights(1, 0, ahead, z == 0)
-            for j in range(parts):
-                local_w(j).start()
-        else:
-            own_weights(0, 0, parts, both(z > 0, last - z == d))
-            own_weights(1, 0, parts, both(z < last, z == d))
-
-    @pl.when(c != 0)
-    def _():
-        for s in range(n):
-            for g in range(kvh):
-                kv_core(s, g).wait_recv()
-
-    def each(e, low, do):
-        ok = both(e >= low, e < steps)
-        d, j = e // parts + 1, e % parts
-        for sign in (-1, 1):
-            s = z + sign * d
-
-            @pl.when(both(ok, both(s >= 0, s < n)))
-            def _(s=s, sign=sign):
-                do(s, j, sign)
+            kv_core(z, g).start()
+
+    def receive(s, g, way):
+        kv_copy(s, g, way, False).wait_recv()
+        to = z + 2 * way - 1
+
+        @pl.when(both(to >= 0, to < n))
+        def _():
+            kv_copy(s, g, way, False).start()
+
+        @pl.when(c == 0)
+        def _():
+            kv_core(s, g).start()
 
     def arrive(s, j, sign):
         way = (1 - sign) // 2
@@ -211,13 +189,8 @@
 
             core_copy(s, j, 0).start()
 
-    def arrive_in_line(s, j, sign):
-        @pl.when(jnp.logical_not(both(is_host, both(s == guest, j >= ahead))))
-        def _():
-            arrive(s, j, sign)
-
-    def pass_on(s, j, sign):
-        @pl.when(both(wanted(z, s, j), jnp.logical_not(whole(s, j))))
+    def pass_on(s, j):
+        @pl.when(wanted(z, s, j))
         def _():
             y_copy(s, j).wait_recv()
             core_copy(s, j, 1).start()
@@ -250,8 +223,8 @@
         core_copy(s, j, 1).wait_recv()
         project(s, j)
 
-    def gather_project(s, j, sign):
-        @pl.when(both(wanted(z, s, j), jnp.logical_not(whole(s, j))))
+    def gather_project(s, j):
+        @pl.when(wanted(z, s, j))
         def _():
             gathered(s, j)
 
@@ -291,9 +264,46 @@
         def _():
             put(lambda span: cbuf[place(z, s, j), span, :].astype(jnp.float32))
 
-    units = spans * kvh
     lag = 2
     lead = per_kv * tok
+    units = spans * kvh
+    pace = max(parts // 6, 1)
+
+    def inner(e):
+        s, j = source(e)
+
+        @pl.when(both(e >= 0, e < length))
+        def _():
+            arrive(s, j, inward)
+
+    def outer(e):
+        @pl.when(both(e >= 0, e < ahead))
+        def _():
+            arrive(guest, e, -inward)
+
+    @pl.when(is_end)
+    def _():
+        for d in range(1, n):
+            for g in range(kvh):
+                receive(z + inward * d, g, way_out)
+
+    @pl.when(is_host)
+    def _():
+        for g in range(kvh):
+            receive(guest, g, way_in)
+            receive(z + inward, g, way_out)
+        own_weights(way_in, 0, parts)
+        for g in range(kvh):
+            receive(z + 2 * inward, g, way_out)
+        own_weights(way_out, 0, keep)
+        for k in range(pace):
+            outer(k)
+
+    @pl.when(c != 0)
+    def _():
+        for s in range(n):
+            for g in range(kvh):
+                kv_core(s, g).wait_recv()
 
     def attend(u, carry):
         i, g = u // kvh, u % kvh
@@ -301,8 +311,8 @@
 
         def fold(k, state):
             top, total, mixed = state
-            keys = kvbuf[k, g, 0].reshape(n * tok, hd)
-            values = kvbuf[k, g, 1].reshape(n * tok, hd)
+            keys = kvbuf[:, g, 0, k].reshape(n * tok, hd)
+            values = kvbuf[:, g, 1, k].reshape(n * tok, hd)
             scores = lax.dot_general(
                 query, keys, (((1,), (1,)), ((), ())), preferred_element_type=jnp.float32
             )
@@ -332,18 +342,25 @@
         def _():
             a_copy(i).start()
 
-        each(u, 0, arrive_in_line)
+        @pl.when(is_host)
+        def _():
+            for k in range(pace):
+                outer((u + 1) * pace + k)
+                inner(u * pace + k)
+
+        @pl.when(both(is_end, c != 0))
+        def _():
+            for k in range(pace):
+                inner((u - 1) * pace + k)
+
         return carry
 
     lax.fori_loop(0, units, attend, 0)
-
-    own_weights(0, ahead, parts, z == last)
-    own_weights(1, ahead, parts, z == 0)
 
     @pl.when(is_end)
     def _():
-        for j in range(late, parts):
-            rest_copy(z, j).start()
+        done = jnp.where(c == 0, 0, min((units - 1) * pace, keep))
+        lax.fori_loop(done, keep, lambda e, carry: (inner(e), carry)[1], 0)
 
     def own(j, carry):
         local_w(j).wait()
@@ -352,18 +369,37 @@
 
     lax.fori_loop(0, parts, own, 0)
 
-    turn = jnp.where(c == 0, 4, 6)
-    shift, due, sums = 4, 2 * parts, 2 * parts
+    turn = jnp.where(c == 0, 3 * pace, 6 * pace)
+    shift, due, sums, go = 4 * pace, 9 * pace, 2 * parts, 3 * pace
 
     def run(e, carry):
-        each(e, units, arrive_in_line)
-        k = e - shift
-
-        @pl.when(both(is_host, both(k >= ahead, k < parts)))
-        def _():
-            arrive(guest, k, -inward)
-
-        each(e - lag, 0, pass_on)
+        @pl.when(both(is_end, e == go))
+        def _():
+            own_weights(way_in, ahead, parts)
+            for j in range(late, parts):
+                rest_copy(z, j).start()
+
+        @pl.when(is_host)
+        def _():
+            @pl.when(e >= units * pace)
+            def _():
+                inner(e)
+
+            k = e - shift
+
+            @pl.when(both(k >= ahead, k < parts))
+            def _():
+                arrive(guest, k, -inward)
+
+        f = e - lag
+
+        @pl.when(both(f >= 0, f < length))
+        def _():
+            pass_on(*source(f))
+
+        @pl.when(both(is_host, both(f >= 0, f < late)))
+        def _():
+            pass_on(guest, f)
 
         @pl.when(both(is_host, e == turn))
         def _():
@@ -371,17 +407,20 @@
                 a_copy(i).wait_recv()
 
             def catch_up(f, carry):
-                project_guest(z + inward * (f // parts), f % parts)
+                project_guest(*source(f - parts))
                 return carry
 
             lax.fori_loop(keep, turn - lag - 1 + parts, catch_up, 0)
 
-        each(e - lag - 1, 0, gather_project)
-        f = e - lag - 1 + parts
-
-        @pl.when(both(both(is_host, e >= turn), f < (n - 1) * parts))
-        def _():
-            project_guest(z + inward * (f // parts), f % parts)
+        f = e - lag - 1
+
+        @pl.when(both(f >= 0, f < length))
+        def _():
+            gather_project(*source(f))
+
+            @pl.when(both(is_host, e >= turn))
+            def _():
+                project_guest(*source(f))
 
         k = e - due + late
 
@@ -390,9 +429,11 @@
             rest_copy(guest, k).wait_recv()
             core_copy(guest, k, 1).start()
 
-        @pl.when(both(is_host, both(k - 1 >= late, k - 1 < parts)))
-        def _():
-            gathered(guest, k - 1)
+        k = jnp.where(f < late, f, k - 1)
+
+        @pl.when(both(is_host, both(k >= 0, jnp.logical_or(f < late, both(k >= late, k < parts)))))
+        def _():
+            gathered(guest, k)
 
         q = e - sums
 
@@ -402,7 +443,9 @@
 
         return carry
 
-    lax.fori_loop(lag, max(steps + lag + 1, due + parts - late + 1, sums + owned * parts), run, 0)
+    lax.fori_loop(
+        lag, max(last * parts + lag + 1, due + parts - late + 1, sums + owned * parts), run, 0
+    )
 
     for s in range(n):
         for way, ok in reach:
@@ -462,10 +505,10 @@
     depth, cols = out_weight.shape
     n, tps, cores = lax.axis_size("seq"), lax.axis_size("tp"), lax.axis_size("span")
     sub, owned, wide = cols // parts, n // tps, noise_table.shape[1]
-    keep, late, ahead = parts // 2, parts // 3, parts - parts // 3
+    keep, late, ahead = 4 * parts // 6, parts // 6, 4 * parts // 6
     extra = (n - 1) * parts - keep
     q = jnp.transpose(queries, (0, 2, 1, 3))
-    kv = jnp.stack([key_states, value_states], axis=0).transpose(1, 3, 0, 2, 4)
+    kv = jnp.stack([key_states, value_states], axis=0).transpose(3, 0, 1, 2, 4)
     vmem = pl.BlockSpec(memory_space=pltpu.VMEM)
     dma = pltpu.SemaphoreType.DMA
     tile = (owned, parts, spans * tok, sub)
@@ -478,7 +521,7 @@
         ],
         out_specs=vmem,
         scratch_shapes=[
-            pltpu.VMEM((spans * cores, kvh, 2, n, tok, hd), jnp.bfloat16),
+            pltpu.VMEM((n, kvh, 2, spans * cores, tok, hd), jnp.bfloat16),
             pltpu.VMEM((n, parts, depth, sub), jnp.bfloat16),
             pltpu.VMEM((2 * spans * tok, depth), jnp.bfloat16),
             pltpu.VMEM(tile, jnp.float32),

time: 107 us -> 98.5 us (0.921); the launches traced: 106 us -> 98.3 us
  Pallas kernels: 101 us -> 93.9 us
    pallas_call x1, Pallas kernels: 101 us -> 93.9 us  [fused(): pl.pallas_call(functools.partial(fused_kernel, parts, keep, late, ahead),...]
where the time goes in v3:
time: 98.5 us; the launch traced here: 98.3 us
  Pallas kernels  93.9 us (95%)
  local copies, waits for them, and re-layouts  3.65 us (4%)
    pallas_call x1, Pallas kernels, fused(): pl.pallas_call(functools.partial(fused_kernel, parts, keep, late, ahead),...  93.9 us
    unnamed x1, local copies, waits for them, and re-layouts  2.65 us

profile of v3, /device:TPU:2, one launch (start us, length us, event | category | flops | bytes accessed | tf_op | source)
XLA Modules:
  0.0 98.3 jit_solution(3104287766069237820)
XLA Ops:
  0.0 1.0 %copy_bitcast_fusion = (bf16[1,2,128,2,128]{4,2,1,0,3:T(8,128)(2,1)S(1)}, bf16[1,2,128,2,128]{4,2,1,0,3:T(8,128)(2,1)S(1)}) fusion(bf16[2,128,2,128]{3,2,1,0:T(2,128)(2,1)} %param.8, bf16[2,128,2,128]{3,2,1,0:T(2,128)(2,1)} %param.7), kind=kLoop, calls=%fused_computation.1 | loop fusion | bytes 524288 | tf_op jit(solution)/shard_map/stack | solution.py:511
  1.0 0.7 maximum_bitcast_fusion.kv_ref
  1.7 93.9 %relay_attention.1 = bf16[256,3072]{1,0:T(8,128)(2,1)} custom-call(s32[4]{0:T(128)} %plan_ref.1, bf16[2,12,128,128]{3,2,1,0:T(8,128)(2,1)} %bitcast.9, bf16[2,2,2,128,128]{4,3,2,1,0:T(8,128)(2,1)} %maximum_bitcast_fusion.kv_ref, f32[64,3072]{1,0:T(8,128)} %noise_ref.1, bf16[1536,1536]{1,0:T(8,128)(2,1)} %w_ref.1), custom_call_target="tpu_custom_call" | custom-call | tf_op jit(solution)/shard_map/relay_attention/pallas_call | solution.py:515
  95.7 2.7 %copy.12 = bf16[2,128,3072]{2,1,0:T(8,128)(2,1)} copy(bf16[2,128,3072]{2,1,0:T(8,128)(2,1)} %bitcast.8) | data formatting | bytes 3145728

commit v4 on v3

--- a/solution.py
+++ b/solution.py
@@ -12,16 +12,17 @@
 
 
 def fused_kernel(
-    parts, keep, late, ahead, plan_ref, q_ref, kv_ref, noise_ref, w_ref, out_ref,
+    parts, keep, late, ahead, plan_ref, q_hbm, kv_ref, noise_hbm, w_ref, out_hbm,
     kvbuf, wbuf, abuf, pbuf, xsend, xbuf, csend, cbuf,
     kv_send, kv_recv, kvc_send, kvc_recv, loc, wz_send, wz_recv, wf_send, wf_recv,
-    wc_send, wc_recv, wy_send, wy_recv, x_send, x_recv, a_send, a_recv, c_send, c_recv,
+    wc_send, wc_recv, wy_send, wy_recv, x_send, x_recv, a_send, a_recv, c_send, c_recv, gates,
+    q_ref, noise_ref, out_ref, out_sem,
 ):
     y, c = lax.axis_index("rep"), lax.axis_index("span")
     z, t = lax.axis_index("seq"), lax.axis_index("tp")
     n = lax.axis_size("seq")
     cores, tps = lax.axis_size("span"), lax.axis_size("tp")
-    spans, heads, tok, hd = q_ref.shape
+    spans, heads, tok, hd = q_hbm.shape
     kvh = kv_ref.shape[0]
     per_kv = heads // kvh
     depth, cols = w_ref.shape
@@ -116,6 +117,18 @@
     def local_w(j):
         return pltpu.make_async_copy(w_ref.at[:, columns(j)], wbuf.at[z, j], loc.at[j])
 
+    def local_q():
+        return pltpu.make_async_copy(q_hbm, q_ref, loc.at[parts + 1])
+
+    def local_noise():
+        return pltpu.make_async_copy(noise_hbm, noise_ref, loc.at[parts + 2])
+
+    def put_copy(s, j):
+        at = pl.ds(pl.multiple_of(lax.rem(s, owned) * cols + j * sub, 128), sub)
+        return pltpu.make_async_copy(
+            out_ref.at[:, at], out_hbm.at[:, at], out_sem.at[lax.rem(s, owned), j]
+        )
+
     def local_kv():
         return pltpu.make_async_copy(
             kv_ref, kvbuf.at[z, :, :, pl.ds(first, spans)], loc.at[parts]
@@ -145,6 +158,8 @@
         for j in range(low, high):
             z_copy(z, j, way, True).start()
 
+    local_q().start()
+    local_noise().start()
     for j in range(parts):
         local_w(j).start()
 
@@ -250,8 +265,7 @@
 
         def put(own):
             for i in range(spans):
-                level = plan_ref[first + i]
-                gate = noise_ref[pl.ds(level, 1), where]
+                gate = gates[i, :, where]
                 span = pl.ds(i * tok, tok)
                 total = own(span) + xbuf[at, j, span, :].astype(jnp.float32)
                 out_ref[span, where] = (total * gate).astype(out_ref.dtype)
@@ -264,7 +278,9 @@
         def _():
             put(lambda span: cbuf[place(z, s, j), span, :].astype(jnp.float32))
 
-    lag = 2
+        put_copy(s, j).start()
+
+    lag = 3
     lead = per_kv * tok
     units = spans * kvh
     pace = max(parts // 6, 1)
@@ -298,6 +314,12 @@
         own_weights(way_out, 0, keep)
         for k in range(pace):
             outer(k)
+            inner(k)
+
+    local_q().wait()
+    local_noise().wait()
+    for i in range(spans):
+        gates[i] = noise_ref[pl.ds(plan_ref[first + i], 1), :]
 
     @pl.when(c != 0)
     def _():
@@ -346,7 +368,7 @@
         def _():
             for k in range(pace):
                 outer((u + 1) * pace + k)
-                inner(u * pace + k)
+                inner((u + 1) * pace + k)
 
         @pl.when(both(is_end, c != 0))
         def _():
@@ -369,7 +391,38 @@
 
     lax.fori_loop(0, parts, own, 0)
 
-    turn = jnp.where(c == 0, 3 * pace, 6 * pace)
+    def drain(f, carry):
+        s, j = source(f - parts)
+        s = jnp.where(s == z + inward * (length // parts + 1), guest, s)
+
+        @pl.when(both(both(z > 0, s >= z), wanted(z - 1, s, j)))
+        def _():
+            z_copy(s, j, 0, False).wait_send()
+
+        @pl.when(both(both(z < last, s <= z), wanted(z + 1, s, j)))
+        def _():
+            z_copy(s, j, 1, False).wait_send()
+
+        @pl.when(both(s != z, wanted(z, s, j)))
+        def _():
+            core_copy(s, j, 0).wait_send()
+            core_copy(s, j, 1).wait_send()
+
+            @pl.when(jnp.logical_not(whole(s, j)))
+            def _():
+                y_copy(s, j).wait_send()
+
+        @pl.when(s // owned != t)
+        def _():
+            x_copy(s, j, xsend.at[lax.rem(s, owned), j]).wait_send()
+
+        @pl.when(both(is_host, jnp.logical_not(wanted(guest, s, j))))
+        def _():
+            c_copy(place(guest, s, j)).wait_send()
+
+        return carry
+
+    turn = jnp.where(c == 0, 4 * pace, 6 * pace)
     shift, due, sums, go = 4 * pace, 9 * pace, 2 * parts, 3 * pace
 
     def run(e, carry):
@@ -381,7 +434,7 @@
 
         @pl.when(is_host)
         def _():
-            @pl.when(e >= units * pace)
+            @pl.when(e > units * pace)
             def _():
                 inner(e)
 
@@ -440,6 +493,7 @@
         @pl.when(both(q >= 0, q < owned * parts))
         def _():
             finish(q)
+            lax.fori_loop(q * tps, (q + 1) * tps, drain, 0)
 
         return carry
 
@@ -466,37 +520,8 @@
         for j in range(late, parts):
             rest_copy(z, j).wait_send()
 
-    def drain(f, carry):
-        s, j = f // parts, f % parts
-
-        @pl.when(both(both(z > 0, s >= z), wanted(z - 1, s, j)))
-        def _():
-            z_copy(s, j, 0, False).wait_send()
-
-        @pl.when(both(both(z < last, s <= z), wanted(z + 1, s, j)))
-        def _():
-            z_copy(s, j, 1, False).wait_send()
-
-        @pl.when(both(s != z, wanted(z, s, j)))
-        def _():
-            core_copy(s, j, 0).wait_send()
-            core_copy(s, j, 1).wait_send()
-
-            @pl.when(jnp.logical_not(whole(s, j)))
-            def _():
-                y_copy(s, j).wait_send()
-
-        @pl.when(s // owned != t)
-        def _():
-            x_copy(s, j, xsend.at[lax.rem(s, owned), j]).wait_send()
-
-        @pl.when(both(is_host, jnp.logical_not(wanted(guest, s, j))))
-        def _():
-            c_copy(place(guest, s, j)).wait_send()
-
-        return carry
-
-    lax.fori_loop(0, n * parts, drain, 0)
+    for q in range(owned * parts):
+        put_copy(mine + q // parts, q % parts).wait()
 
 
 def fused(parts, queries, key_states, value_states, out_weight, noise_table, plan):
@@ -509,17 +534,16 @@
     extra = (n - 1) * parts - keep
     q = jnp.transpose(queries, (0, 2, 1, 3))
     kv = jnp.stack([key_states, value_states], axis=0).transpose(3, 0, 1, 2, 4)
-    vmem = pl.BlockSpec(memory_space=pltpu.VMEM)
+    where_it_is = pl.BlockSpec(memory_space=pl.ANY)
     dma = pltpu.SemaphoreType.DMA
     tile = (owned, parts, spans * tok, sub)
     out = pl.pallas_call(
         functools.partial(fused_kernel, parts, keep, late, ahead),
         out_shape=jax.ShapeDtypeStruct((spans * tok, wide), jnp.bfloat16),
         in_specs=[
-            pl.BlockSpec(memory_space=pltpu.SMEM), vmem, vmem, vmem,
-            pl.BlockSpec(memory_space=pl.ANY),
+            pl.BlockSpec(memory_space=pltpu.SMEM), where_it_is, where_it_is, where_it_is, where_it_is,
         ],
-        out_specs=vmem,
+        out_specs=where_it_is,
         scratch_shapes=[
             pltpu.VMEM((n, kvh, 2, spans * cores, tok, hd), jnp.bfloat16),
             pltpu.VMEM((n, parts, depth, sub), jnp.bfloat16),
@@ -529,11 +553,16 @@
             pltpu.VMEM(tile, jnp.bfloat16),
             pltpu.VMEM((extra, spans * tok, sub), jnp.bfloat16),
             pltpu.VMEM((extra, spans * tok, sub), jnp.bfloat16),
-            dma((2, n, kvh)), dma((n, kvh)), dma((n, kvh)), dma((n, kvh)), dma((parts + 1,)),
+            dma((2, n, kvh)), dma((n, kvh)), dma((n, kvh)), dma((n, kvh)), dma((parts + 3,)),
             dma((2, n, parts)), dma((n, parts)), dma((parts,)), dma((parts,)),
             dma((2, n, parts)), dma((2, n, parts)), dma((n, parts)), dma((n, parts)),
             dma((owned, parts)), dma((owned, parts)), dma((spans,)), dma((spans,)),
             dma((extra,)), dma((extra,)),
+            pltpu.VMEM((spans, 1, wide), jnp.float32),
+            pltpu.VMEM(q.shape, q.dtype),
+            pltpu.VMEM(noise_table.shape, noise_table.dtype),
+            pltpu.VMEM((spans * tok, wide), jnp.bfloat16),
+            dma((owned, parts)),
         ],
         compiler_params=pltpu.CompilerParams(
             collective_id=0, has_side_effects=True, vmem_limit_bytes=60 * 1024 * 1024

time: 98.5 us -> 96.1 us (0.976)
  Pallas kernels: 93.9 us -> 91.5 us
    pallas_call x1, Pallas kernels: 93.9 us -> 91.5 us  [fused(): pl.pallas_call(functools.partial(fused_kernel, parts, keep, late, ahead),...]
where the time goes in v4:
time: 96.1 us; the launch traced here: 95.9 us
  Pallas kernels  91.5 us (95%)
  local copies, waits for them, and re-layouts  3.65 us (4%)
    pallas_call x1, Pallas kernels, fused(): pl.pallas_call(functools.partial(fused_kernel, parts, keep, late, ahead),...  91.5 us
    unnamed x1, local copies, waits for them, and re-layouts  2.65 us

profile of v4, /device:TPU:2, one launch (start us, length us, event | category | flops | bytes accessed | tf_op | source)
XLA Modules:
  0.0 95.9 jit_solution(11204934625953903465)
XLA Ops:
  0.0 1.0 %copy_bitcast_fusion = (bf16[1,2,128,2,128]{4,2,1,0,3:T(8,128)(2,1)S(1)}, bf16[1,2,128,2,128]{4,2,1,0,3:T(8,128)(2,1)S(1)}) fusion(bf16[2,128,2,128]{3,2,1,0:T(2,128)(2,1)} %param.8, bf16[2,128,2,128]{3,2,1,0:T(2,128)(2,1)} %param.7), kind=kLoop, calls=%fused_computation.1 | loop fusion | bytes 524288 | tf_op jit(solution)/shard_map/stack | solution.py:536
  1.0 0.7 maximum_bitcast_fusion.kv_ref
  1.7 91.5 %relay_attention.1 = bf16[256,3072]{1,0:T(8,128)(2,1)} custom-call(s32[4]{0:T(128)} %plan_ref.1, bf16[2,12,128,128]{3,2,1,0:T(8,128)(2,1)} %bitcast.9, bf16[2,2,2,128,128]{4,3,2,1,0:T(8,128)(2,1)} %maximum_bitcast_fusion.kv_ref, f32[64,3072]{1,0:T(8,128)} %noise_hbm.1, bf16[1536,1536]{1,0:T(8,128)(2,1)} %w_ref.1), custom_call_target="tpu_custom_call" | custom-call | tf_op jit(solution)/shard_map/relay_attention/pallas_call | solution.py:540
  93.3 2.7 %copy.12 = bf16[2,128,3072]{2,1,0:T(8,128)(2,1)} copy(bf16[2,128,3072]{2,1,0:T(8,128)(2,1)} %bitcast.8) | data formatting | bytes 3145728

commit v5 on v4

--- a/solution.py
+++ b/solution.py
@@ -68,70 +68,93 @@
             device_id=where, device_id_type=MESH,
         )
 
+    def turn_of(r, s, j):
+        inside = (s - r) * jnp.where(2 * r < n, 1, -1) > 0
+        return jnp.where(inside, (jnp.abs(s - r) - 1) * parts, (n - 2) * parts) + j
+
+    def sent(part, sem):
+        remote(part, part, sem, sem, {"span": 1 - c}).wait_send()
+
     def z_copy(s, j, way, own):
         dst = wbuf.at[s, j, rows(y, c)]
         src = w_ref.at[rows(y, c), columns(j)] if own else dst
         to = z + 2 * way - 1
-        return remote(src, dst, wz_send.at[way, s, j], wz_recv.at[s, j], {"seq": to})
+        group = jnp.where(way == way_in, 0, 1) if own else 2
+        return remote(src, dst, wz_send.at[group], wz_recv.at[turn_of(to, s, j)], {"seq": to})
+
+    def z_arrival(s, j):
+        dst = wbuf.at[s, j, rows(y, c)]
+        return remote(dst, dst, wz_send.at[2], wz_recv.at[turn_of(z, s, j)], {"seq": z + inward})
 
     def rest_copy(s, j):
         src = w_ref.at[rows(1 - y, c), columns(j)]
         return remote(
-            src, wbuf.at[s, j, rows(1 - y, c)], wf_send.at[j], wf_recv.at[j], {"seq": z + inward}
+            src, wbuf.at[s, j, rows(1 - y, c)], wf_send, wf_recv.at[j], {"seq": z + inward}
         )
 
     def core_copy(s, j, kind):
         part = wbuf.at[s, j, rows(y if kind == 0 else 1 - y, c)]
-        return remote(part, part, wc_send.at[kind, s, j], wc_recv.at[kind, s, j], {"span": 1 - c})
+        return remote(part, part, wc_send, wc_recv.at[turn_of(z, s, j)], {"span": 1 - c})
+
+    def core_arrival(s, j):
+        part = wbuf.at[s, j, pl.ds(0, 2 * quarter)]
+        return remote(part, part, wc_send, wc_recv.at[turn_of(z, s, j)], {"span": 1 - c})
 
     def y_copy(s, j):
         part = wbuf.at[s, j, rows(y, c)]
-        return remote(part, part, wy_send.at[s, j], wy_recv.at[s, j], {"rep": 1 - y})
+        group = jnp.where(both(is_host, s == guest), 1, 0)
+        return remote(
+            part, part, wy_send.at[group], wy_recv.at[turn_of(z, s, j)], {"rep": 1 - y}
+        )
 
     def x_copy(s, j, src):
         at = lax.rem(s, owned)
         return remote(
-            src, xbuf.at[at, j], x_send.at[at, j], x_recv.at[at, j], {"tp": 1 - t}
+            src, xbuf.at[at, j], x_send, x_recv.at[at, j], {"tp": 1 - t}
         )
 
     def a_copy(i):
         src = abuf.at[pl.ds(pl.multiple_of(i * tok, tok), tok)]
         dst = abuf.at[pl.ds(pl.multiple_of(rows_own + i * tok, tok), tok)]
-        return remote(src, dst, a_send.at[i], a_recv.at[i], {"seq": z + inward})
+        return remote(src, dst, a_send, a_recv, {"seq": z + inward})
 
     def c_copy(f):
         return remote(
-            csend.at[f], cbuf.at[f], c_send.at[f], c_recv.at[f], {"seq": z - inward}
+            csend.at[f], cbuf.at[f], c_send, c_recv.at[f], {"seq": z - inward}
         )
 
     def kv_copy(s, g, way, own):
         dst = kvbuf.at[s, g, :, pl.ds(first, spans)]
         src = kv_ref.at[g] if own else dst
         to = z + 2 * way - 1
-        return remote(src, dst, kv_send.at[way, s, g], kv_recv.at[s, g], {"seq": to})
+        group = jnp.where(way == way_in, 0, 1)
+        return remote(src, dst, kv_send.at[group], kv_recv.at[s, g], {"seq": to})
 
     def kv_core(s, g):
         part = kvbuf.at[s, g, :, pl.ds(0, spans)]
-        return remote(part, part, kvc_send.at[s, g], kvc_recv.at[s, g], {"span": 1 - c})
+        return remote(part, part, kvc_send, kvc_recv, {"span": 1 - c})
 
     def local_w(j):
-        return pltpu.make_async_copy(w_ref.at[:, columns(j)], wbuf.at[z, j], loc.at[j])
+        return pltpu.make_async_copy(w_ref.at[:, columns(j)], wbuf.at[z, j], loc.at[3])
+
+    def all_w():
+        return pltpu.make_async_copy(wbuf.at[z], wbuf.at[z], loc.at[3])
 
     def local_q():
-        return pltpu.make_async_copy(q_hbm, q_ref, loc.at[parts + 1])
+        return pltpu.make_async_copy(q_hbm, q_ref, loc.at[1])
 
     def local_noise():
-        return pltpu.make_async_copy(noise_hbm, noise_ref, loc.at[parts + 2])
+        return pltpu.make_async_copy(noise_hbm, noise_ref, loc.at[2])
 
     def put_copy(s, j):
         at = pl.ds(pl.multiple_of(lax.rem(s, owned) * cols + j * sub, 128), sub)
         return pltpu.make_async_copy(
-            out_ref.at[:, at], out_hbm.at[:, at], out_sem.at[lax.rem(s, owned), j]
+            out_ref.at[:, at], out_hbm.at[:, at], out_sem
         )
 
     def local_kv():
         return pltpu.make_async_copy(
-            kv_ref, kvbuf.at[z, :, :, pl.ds(first, spans)], loc.at[parts]
+            kv_ref, kvbuf.at[z, :, :, pl.ds(first, spans)], loc.at[0]
         )
 
     reach = ((0, z > 0), (1, z < last))
@@ -192,7 +215,7 @@
 
         @pl.when(wanted(z, s, j))
         def _():
-            z_copy(s, j, way, False).wait_recv()
+            z_arrival(s, j).wait_recv()
 
             @pl.when(both(both(onward >= 0, onward < n), wanted(onward, s, j)))
             def _():
@@ -234,8 +257,7 @@
         c_copy(f).start()
 
     def gathered(s, j):
-        core_copy(s, j, 0).wait_recv()
-        core_copy(s, j, 1).wait_recv()
+        core_arrival(s, j).wait_recv()
         project(s, j)
 
     def gather_project(s, j):
@@ -323,9 +345,8 @@
 
     @pl.when(c != 0)
     def _():
-        for s in range(n):
-            for g in range(kvh):
-                kv_core(s, g).wait_recv()
+        kv_all = kvbuf.at[:, :, :, pl.ds(0, spans)]
+        remote(kv_all, kv_all, kvc_send, kvc_recv, {"span": 1 - c}).wait_recv()
 
     def attend(u, carry):
         i, g = u // kvh, u % kvh
@@ -385,42 +406,11 @@
         lax.fori_loop(done, keep, lambda e, carry: (inner(e), carry)[1], 0)
 
     def own(j, carry):
-        local_w(j).wait()
         project(z, j)
         return carry
 
+    all_w().wait()
     lax.fori_loop(0, parts, own, 0)
-
-    def drain(f, carry):
-        s, j = source(f - parts)
-        s = jnp.where(s == z + inward * (length // parts + 1), guest, s)
-
-        @pl.when(both(both(z > 0, s >= z), wanted(z - 1, s, j)))
-        def _():
-            z_copy(s, j, 0, False).wait_send()
-
-        @pl.when(both(both(z < last, s <= z), wanted(z + 1, s, j)))
-        def _():
-            z_copy(s, j, 1, False).wait_send()
-
-        @pl.when(both(s != z, wanted(z, s, j)))
-        def _():
-            core_copy(s, j, 0).wait_send()
-            core_copy(s, j, 1).wait_send()
-
-            @pl.when(jnp.logical_not(whole(s, j)))
-            def _():
-                y_copy(s, j).wait_send()
-
-        @pl.when(s // owned != t)
-        def _():
-            x_copy(s, j, xsend.at[lax.rem(s, owned), j]).wait_send()
-
-        @pl.when(both(is_host, jnp.logical_not(wanted(guest, s, j))))
-        def _():
-            c_copy(place(guest, s, j)).wait_send()
-
-        return carry
 
     turn = jnp.where(c == 0, 4 * pace, 6 * pace)
     shift, due, sums, go = 4 * pace, 9 * pace, 2 * parts, 3 * pace
@@ -456,8 +446,8 @@
 
         @pl.when(both(is_host, e == turn))
         def _():
-            for i in range(spans):
-                a_copy(i).wait_recv()
+            rows_in = abuf.at[pl.ds(rows_own, rows_own)]
+            remote(rows_in, rows_in, a_send, a_recv, {"seq": guest}).wait_recv()
 
             def catch_up(f, carry):
                 project_guest(*source(f - parts))
@@ -493,7 +483,6 @@
         @pl.when(both(q >= 0, q < owned * parts))
         def _():
             finish(q)
-            lax.fori_loop(q * tps, (q + 1) * tps, drain, 0)
 
         return carry
 
@@ -501,27 +490,36 @@
         lag, max(last * parts + lag + 1, due + parts - late + 1, sums + owned * parts), run, 0
     )
 
-    for s in range(n):
-        for way, ok in reach:
-            @pl.when(both(ok, (z <= s) if way == 0 else (z >= s)))
-            def _(s=s, way=way):
-                for g in range(kvh):
-                    kv_copy(s, g, way, False).wait_send()
-
-        @pl.when(c == 0)
-        def _(s=s):
-            for g in range(kvh):
-                kv_core(s, g).wait_send()
+    piece = pl.ds(0, quarter)
+    pair = pl.ds(0, 2 * quarter)
 
     @pl.when(is_end)
     def _():
-        for i in range(spans):
-            a_copy(i).wait_send()
-        for j in range(late, parts):
-            rest_copy(z, j).wait_send()
-
-    for q in range(owned * parts):
-        put_copy(mine + q // parts, q % parts).wait()
+        sent(kv_ref, kv_send.at[0])
+        sent(w_ref.at[piece], wz_send.at[0])
+        sent(w_ref.at[piece, pl.ds(0, (parts - late) * sub)], wf_send)
+        sent(wbuf.at[0, pl.ds(0, keep), pair], wc_send)
+        sent(wbuf.at[0, pl.ds(0, keep), piece], wy_send.at[0])
+        sent(abuf.at[pl.ds(0, rows_own)], a_send)
+
+    @pl.when(is_host)
+    def _():
+        sent(kvbuf.at[pl.ds(0, 2), :, :, pl.ds(0, spans)], kv_send.at[0])
+        sent(kvbuf.at[pl.ds(0, n - 1), :, :, pl.ds(0, spans)], kv_send.at[1])
+        sent(w_ref.at[piece], wz_send.at[0])
+        sent(w_ref.at[piece, pl.ds(0, keep * sub)], wz_send.at[1])
+        sent(wbuf.at[0, :, piece], wz_send.at[2])
+        sent(wbuf.at[pl.ds(0, n - 1), :, pair], wc_send)
+        sent(wbuf.at[pl.ds(0, n - 2), :, piece], wy_send.at[0])
+        sent(w_ref.at[piece, pl.ds(0, late * sub)], wy_send.at[1])
+        sent(csend, c_send)
+
+    @pl.when(c == 0)
+    def _():
+        sent(kvbuf.at[:, :, :, pl.ds(0, spans)], kvc_send)
+
+    sent(xsend, x_send)
+    pltpu.make_async_copy(out_ref, out_hbm, out_sem).wait()
 
 
 def fused(parts, queries, key_states, value_states, out_weight, noise_table, plan):
@@ -531,7 +529,7 @@
     n, tps, cores = lax.axis_size("seq"), lax.axis_size("tp"), lax.axis_size("span")
     sub, owned, wide = cols // parts, n // tps, noise_table.shape[1]
     keep, late, ahead = 4 * parts // 6, parts // 6, 4 * parts // 6
-    extra = (n - 1) * parts - keep
+    extra, taken = (n - 1) * parts - keep, (n - 1) * parts
     q = jnp.transpose(queries, (0, 2, 1, 3))
     kv = jnp.stack([key_states, value_states], axis=0).transpose(3, 0, 1, 2, 4)
     where_it_is = pl.BlockSpec(memory_space=pl.ANY)
@@ -553,16 +551,15 @@
             pltpu.VMEM(tile, jnp.bfloat16),
             pltpu.VMEM((extra, spans * tok, sub), jnp.bfloat16),
             pltpu.VMEM((extra, spans * tok, sub), jnp.bfloat16),
-            dma((2, n, kvh)), dma((n, kvh)), dma((n, kvh)), dma((n, kvh)), dma((parts + 3,)),
-            dma((2, n, parts)), dma((n, parts)), dma((parts,)), dma((parts,)),
-            dma((2, n, parts)), dma((2, n, parts)), dma((n, parts)), dma((n, parts)),
-            dma((owned, parts)), dma((owned, parts)), dma((spans,)), dma((spans,)),
-            dma((extra,)), dma((extra,)),
+            dma((2,)), dma((n, kvh)), dma, dma, dma((4,)),
+            dma((3,)), dma((taken,)), dma, dma((parts,)),
+            dma, dma((taken,)), dma((2,)), dma((taken,)),
+            dma, dma((owned, parts)), dma, dma, dma, dma((extra,)),
             pltpu.VMEM((spans, 1, wide), jnp.float32),
             pltpu.VMEM(q.shape, q.dtype),
             pltpu.VMEM(noise_table.shape, noise_table.dtype),
             pltpu.VMEM((spans * tok, wide), jnp.bfloat16),
-            dma((owned, parts)),
+            dma,
         ],
         compiler_params=pltpu.CompilerParams(
             collective_id=0, has_side_effects=True, vmem_limit_bytes=60 * 1024 * 1024

time: 96.1 us -> 94 us (0.978)
  Pallas kernels: 91.5 us -> 89.4 us
    pallas_call x1, Pallas kernels: 91.5 us -> 89.4 us  [fused(): pl.pallas_call(functools.partial(fused_kernel, parts, keep, late, ahead),...]
where the time goes in v5:
time: 94 us; the launch traced here: 93.8 us
  Pallas kernels  89.4 us (95%)
  local copies, waits for them, and re-layouts  3.65 us (4%)
    pallas_call x1, Pallas kernels, fused(): pl.pallas_call(functools.partial(fused_kernel, parts, keep, late, ahead),...  89.4 us
    unnamed x1, local copies, waits for them, and re-layouts  2.65 us

profile of v5, /device:TPU:2, one launch (start us, length us, event | category | flops | bytes accessed | tf_op | source)
XLA Modules:
  0.0 93.8 jit_solution(13731227732360889498)
XLA Ops:
  0.0 1.0 %copy_bitcast_fusion = (bf16[1,2,128,2,128]{4,2,1,0,3:T(8,128)(2,1)S(1)}, bf16[1,2,128,2,128]{4,2,1,0,3:T(8,128)(2,1)S(1)}) fusion(bf16[2,128,2,128]{3,2,1,0:T(2,128)(2,1)} %param.8, bf16[2,128,2,128]{3,2,1,0:T(2,128)(2,1)} %param.7), kind=kLoop, calls=%fused_computation.1 | loop fusion | bytes 524288 | tf_op jit(solution)/shard_map/stack | solution.py:534
  1.0 0.7 maximum_bitcast_fusion.kv_ref
  1.7 89.4 %relay_attention.1 = bf16[256,3072]{1,0:T(8,128)(2,1)} custom-call(s32[4]{0:T(128)} %plan_ref.1, bf16[2,12,128,128]{3,2,1,0:T(8,128)(2,1)} %bitcast.9, bf16[2,2,2,128,128]{4,3,2,1,0:T(8,128)(2,1)} %maximum_bitcast_fusion.kv_ref, f32[64,3072]{1,0:T(8,128)} %noise_hbm.1, bf16[1536,1536]{1,0:T(8,128)(2,1)} %w_ref.1), custom_call_target="tpu_custom_call" | custom-call | tf_op jit(solution)/shard_map/relay_attention/pallas_call | solution.py:538
  91.2 2.7 %copy.12 = bf16[2,128,3072]{2,1,0:T(8,128)(2,1)} copy(bf16[2,128,3072]{2,1,0:T(8,128)(2,1)} %bitcast.8) | data formatting | bytes 3145728

commit v6 on v5

--- a/solution.py
+++ b/solution.py
@@ -12,11 +12,12 @@
 
 
 def fused_kernel(
-    parts, keep, late, ahead, plan_ref, q_hbm, kv_ref, noise_hbm, w_ref, out_hbm,
+    parts, keep, late, ahead, pick, plan_ref, q_hbm, kv_ref, noise_hbm, w_ref, out_hbm,
     kvbuf, wbuf, abuf, pbuf, xsend, xbuf, csend, cbuf,
     kv_send, kv_recv, kvc_send, kvc_recv, loc, wz_send, wz_recv, wf_send, wf_recv,
     wc_send, wc_recv, wy_send, wy_recv, x_send, x_recv, a_send, a_recv, c_send, c_recv, gates,
     q_ref, noise_ref, out_ref, out_sem,
+    gsend, grecv, gpart, g_send, g_recv,
 ):
     y, c = lax.axis_index("rep"), lax.axis_index("span")
     z, t = lax.axis_index("seq"), lax.axis_index("tp")
@@ -53,6 +54,17 @@
         far = place(r, s, j) >= 0
         return jnp.logical_not(both(jnp.logical_or(r == 0, r == last), far))
 
+    shared = parts - keep
+
+    def summed(r, s, j):
+        f = place(r, s, j) + keep
+        k = f - parts - pick
+        return jnp.logical_or(both(f >= keep, f < parts), both(k >= 0, k < shared))
+
+    def sum_at(r, s, j):
+        f = place(r, s, j) + keep
+        return jnp.where(f < parts, f - keep, f - parts - pick)
+
     def whole(s, j):
         return both(is_host, both(s == guest, j >= late))
 
@@ -122,6 +134,9 @@
         return remote(
             csend.at[f], cbuf.at[f], c_send, c_recv.at[f], {"seq": z - inward}
         )
+
+    def g_copy(k):
+        return remote(gsend.at[k], grecv.at[k], g_send, g_recv.at[k], {"tp": 1 - t})
 
     def kv_copy(s, g, way, own):
         dst = kvbuf.at[s, g, :, pl.ds(first, spans)]
@@ -253,8 +268,34 @@
             abuf[pl.ds(rows_own, rows_own)], wbuf[s, j], preferred_element_type=jnp.float32
         )
         f = place(guest, s, j)
-        csend[f] = part.astype(jnp.bfloat16)
-        c_copy(f).start()
+        k = sum_at(guest, s, j)
+        add = summed(guest, s, j)
+        mine = s // owned == t
+
+        @pl.when(jnp.logical_not(add))
+        def _():
+            csend[f] = part.astype(jnp.bfloat16)
+            c_copy(f).start()
+
+        @pl.when(both(add, mine))
+        def _():
+            gpart[k] = part
+
+        @pl.when(both(add, jnp.logical_not(mine)))
+        def _():
+            gsend[k] = part.astype(jnp.bfloat16)
+            g_copy(k).start()
+
+    def pass_sum(f):
+        s, j = source(f - parts)
+
+        @pl.when(s // owned == t)
+        def _():
+            f = place(guest, s, j)
+            k = sum_at(guest, s, j)
+            g_copy(k).wait_recv()
+            csend[f] = (gpart[k] + grecv[k].astype(jnp.float32)).astype(jnp.bfloat16)
+            c_copy(f).start()
 
     def gathered(s, j):
         core_arrival(s, j).wait_recv()
@@ -265,7 +306,7 @@
         def _():
             gathered(s, j)
 
-        @pl.when(jnp.logical_not(wanted(z, s, j)))
+        @pl.when(jnp.logical_not(jnp.logical_or(wanted(z, s, j), summed(z, s, j))))
         def _():
             f = place(z, s, j)
             c_copy(f).wait_recv()
@@ -282,27 +323,45 @@
     def finish(q):
         s, j = jnp.where(q < parts, front, rear), lax.rem(q, parts)
         at = lax.rem(s, owned)
-        x_copy(s, j, xsend.at[at, j]).wait_recv()
+        whole_sum = both(is_end, summed(z, s, j))
+
+        @pl.when(whole_sum)
+        def _():
+            c_copy(place(z, s, j)).wait_recv()
+
+        @pl.when(jnp.logical_not(whole_sum))
+        def _():
+            x_copy(s, j, xsend.at[at, j]).wait_recv()
+
         where = pl.ds(pl.multiple_of(at * cols + j * sub, 128), sub)
 
-        def put(own):
+        def put(total):
             for i in range(spans):
-                gate = gates[i, :, where]
                 span = pl.ds(i * tok, tok)
-                total = own(span) + xbuf[at, j, span, :].astype(jnp.float32)
-                out_ref[span, where] = (total * gate).astype(out_ref.dtype)
+                out_ref[span, where] = (total(span) * gates[i, :, where]).astype(out_ref.dtype)
+
+        def other(span):
+            return xbuf[at, j, span, :].astype(jnp.float32)
+
+        def guests(span):
+            return cbuf[place(z, s, j), span, :].astype(jnp.float32)
 
         @pl.when(wanted(z, s, j))
         def _():
-            put(lambda span: pbuf[at, j, span, :])
-
-        @pl.when(jnp.logical_not(wanted(z, s, j)))
-        def _():
-            put(lambda span: cbuf[place(z, s, j), span, :].astype(jnp.float32))
+            put(lambda span: pbuf[at, j, span, :] + other(span))
+
+        @pl.when(whole_sum)
+        def _():
+            put(guests)
+
+        @pl.when(jnp.logical_not(jnp.logical_or(wanted(z, s, j), whole_sum)))
+        def _():
+            put(lambda span: guests(span) + other(span))
 
         put_copy(s, j).start()
 
-    lag = 3
+    lag, most = 2, 3
+    gap = jnp.where(c == 0, 2, 3)
     lead = per_kv * tok
     units = spans * kvh
     pace = max(parts // 6, 1)
@@ -347,6 +406,15 @@
     def _():
         kv_all = kvbuf.at[:, :, :, pl.ds(0, spans)]
         remote(kv_all, kv_all, kvc_send, kvc_recv, {"span": 1 - c}).wait_recv()
+
+    def relay_in(e):
+        @pl.when(both(e >= 0, e < length))
+        def _():
+            pass_on(*source(e))
+
+        @pl.when(both(is_host, both(e >= 0, e < late)))
+        def _():
+            pass_on(guest, e)
 
     def attend(u, carry):
         i, g = u // kvh, u % kvh
@@ -390,6 +458,7 @@
             for k in range(pace):
                 outer((u + 1) * pace + k)
                 inner((u + 1) * pace + k)
+                relay_in((u + 1) * pace + k - lag)
 
         @pl.when(both(is_end, c != 0))
         def _():
@@ -410,10 +479,10 @@
         return carry
 
     all_w().wait()
-    lax.fori_loop(0, parts, own, 0)
+    lax.fori_loop(0, jnp.where(is_end, parts, 0), own, 0)
 
     turn = jnp.where(c == 0, 4 * pace, 6 * pace)
-    shift, due, sums, go = 4 * pace, 9 * pace, 2 * parts, 3 * pace
+    shift, due, sums, go, own_at = 4 * pace, 9 * pace, 2 * parts, 3 * pace, 5 * pace
 
     def run(e, carry):
         @pl.when(both(is_end, e == go))
@@ -434,15 +503,9 @@
             def _():
                 arrive(guest, k, -inward)
 
-        f = e - lag
-
-        @pl.when(both(f >= 0, f < length))
-        def _():
-            pass_on(*source(f))
-
-        @pl.when(both(is_host, both(f >= 0, f < late)))
-        def _():
-            pass_on(guest, f)
+        @pl.when(jnp.logical_or(is_end, e > units * pace))
+        def _():
+            relay_in(e - lag)
 
         @pl.when(both(is_host, e == turn))
         def _():
@@ -453,9 +516,9 @@
                 project_guest(*source(f - parts))
                 return carry
 
-            lax.fori_loop(keep, turn - lag - 1 + parts, catch_up, 0)
-
-        f = e - lag - 1
+            lax.fori_loop(keep, turn - gap + parts, catch_up, 0)
+
+        f = e - gap
 
         @pl.when(both(f >= 0, f < length))
         def _():
@@ -465,6 +528,22 @@
             def _():
                 project_guest(*source(f))
 
+        @pl.when(both(is_host, e == turn + 2 * pace))
+        def _():
+            lax.fori_loop(keep, parts, lambda f, carry: (pass_sum(f), carry)[1], 0)
+
+        k = e - gap - 2 * pace - pick
+
+        @pl.when(both(is_host, both(k >= 0, k < shared)))
+        def _():
+            pass_sum(parts + pick + k)
+
+        k = e - own_at
+
+        @pl.when(both(is_host, both(k >= 0, k < parts)))
+        def _():
+            project(z, k)
+
         k = e - due + late
 
         @pl.when(both(is_host, both(k >= late, k < parts)))
@@ -487,7 +566,7 @@
         return carry
 
     lax.fori_loop(
-        lag, max(last * parts + lag + 1, due + parts - late + 1, sums + owned * parts), run, 0
+        2, max(last * parts + most, due + parts - late + 1, sums + owned * parts), run, 0
     )
 
     piece = pl.ds(0, quarter)
@@ -501,6 +580,7 @@
         sent(wbuf.at[0, pl.ds(0, keep), pair], wc_send)
         sent(wbuf.at[0, pl.ds(0, keep), piece], wy_send.at[0])
         sent(abuf.at[pl.ds(0, rows_own)], a_send)
+        sent(csend.at[pl.ds(0, owned * parts - shared)], x_send)
 
     @pl.when(is_host)
     def _():
@@ -512,13 +592,14 @@
         sent(wbuf.at[pl.ds(0, n - 1), :, pair], wc_send)
         sent(wbuf.at[pl.ds(0, n - 2), :, piece], wy_send.at[0])
         sent(w_ref.at[piece, pl.ds(0, late * sub)], wy_send.at[1])
-        sent(csend, c_send)
+        sent(csend.at[pl.ds(0, csend.shape[0] - shared)], c_send)
+        sent(gsend, g_send)
+        sent(xsend, x_send)
 
     @pl.when(c == 0)
     def _():
         sent(kvbuf.at[:, :, :, pl.ds(0, spans)], kvc_send)
 
-    sent(xsend, x_send)
     pltpu.make_async_copy(out_ref, out_hbm, out_sem).wait()
 
 
@@ -529,17 +610,19 @@
     n, tps, cores = lax.axis_size("seq"), lax.axis_size("tp"), lax.axis_size("span")
     sub, owned, wide = cols // parts, n // tps, noise_table.shape[1]
     keep, late, ahead = 4 * parts // 6, parts // 6, 4 * parts // 6
+    pick, shared = keep, parts - keep
     extra, taken = (n - 1) * parts - keep, (n - 1) * parts
     q = jnp.transpose(queries, (0, 2, 1, 3))
     kv = jnp.stack([key_states, value_states], axis=0).transpose(3, 0, 1, 2, 4)
     where_it_is = pl.BlockSpec(memory_space=pl.ANY)
+    far = pl.BlockSpec(memory_space=pltpu.HBM)
     dma = pltpu.SemaphoreType.DMA
     tile = (owned, parts, spans * tok, sub)
     out = pl.pallas_call(
-        functools.partial(fused_kernel, parts, keep, late, ahead),
+        functools.partial(fused_kernel, parts, keep, late, ahead, pick),
         out_shape=jax.ShapeDtypeStruct((spans * tok, wide), jnp.bfloat16),
         in_specs=[
-            pl.BlockSpec(memory_space=pltpu.SMEM), where_it_is, where_it_is, where_it_is, where_it_is,
+            pl.BlockSpec(memory_space=pltpu.SMEM), far, where_it_is, far, far,
         ],
         out_specs=where_it_is,
         scratch_shapes=[
@@ -560,9 +643,13 @@
             pltpu.VMEM(noise_table.shape, noise_table.dtype),
             pltpu.VMEM((spans * tok, wide), jnp.bfloat16),
             dma,
+            pltpu.VMEM((shared, spans * tok, sub), jnp.bfloat16),
+            pltpu.VMEM((shared, spans * tok, sub), jnp.bfloat16),
+            pltpu.VMEM((shared, spans * tok, sub), jnp.float32),
+            dma, dma((shared,)),
         ],
         compiler_params=pltpu.CompilerParams(
-            collective_id=0, has_side_effects=True, vmem_limit_bytes=60 * 1024 * 1024
+            collective_id=0, has_side_effects=True, vmem_limit_bytes=48 * 1024 * 1024
         ),
         name="relay_attention",
     )(plan, q, kv, noise_table, out_weight)

time: 94 us -> 89.6 us (0.953)
  Pallas kernels: 89.4 us -> 84.8 us
    pallas_call x1, Pallas kernels: 89.4 us -> 84.8 us  [fused(): pl.pallas_call(functools.partial(fused_kernel, parts, keep, late, ahead,...]
    unnamed x1 -> x7, local copies, waits for them, and re-layouts: 2.65 us -> 3.08 us
where the time goes in v6:
time: 89.6 us; the launch traced here: 89 us
  Pallas kernels  84.8 us (95%)
  local copies, waits for them, and re-layouts  4.15 us (5%)
    pallas_call x1, Pallas kernels, fused(): pl.pallas_call(functools.partial(fused_kernel, parts, keep, late, ahead,...  84.8 us
    unnamed x7, local copies, waits for them, and re-layouts  3.08 us

profile of v6, /device:TPU:2, one launch (start us, length us, event | category | flops | bytes accessed | tf_op | source)
XLA Modules:
  0.0 89.0 jit_solution(5781035105077789440)
XLA Ops:
  0.0 0.0 copy-start
  0.0 1.1 %copy_bitcast_fusion = (bf16[1,2,128,2,128]{4,2,1,0,3:T(8,128)(2,1)S(1)}, bf16[1,2,128,2,128]{4,2,1,0,3:T(8,128)(2,1)S(1)}) fusion(bf16[2,128,2,128]{3,2,1,0:T(2,128)(2,1)} %param.8, bf16[2,128,2,128]{3,2,1,0:T(2,128)(2,1)} %param.7), kind=kLoop, calls=%fused_computation.1 | loop fusion | bytes 524288 | tf_op jit(solution)/shard_map/stack | solution.py:616
  1.1 0.1 copy-done
  1.3 0.0 copy-start.1
  1.3 1.1 %copy-done.1 = f32[64,3072]{1,0:T(8,128)S(1)} copy-done((f32[64,3072]{1,0:T(8,128)S(1)}, f32[64,3072]{1,0:T(8,128)}, u32[]{:S(2)}) %copy-start.1) | copy-done | bytes 786456
  2.4 0.0 copy-start.2
  2.4 0.7 copy-done.2
  3.0 84.8 %relay_attention.1 = bf16[256,3072]{1,0:T(8,128)(2,1)S(1)} custom-call(s32[4]{0:T(128)S(1)} %copy-done.2, bf16[2,12,128,128]{3,2,1,0:T(8,128)(2,1)S(1)} %bitcast.9, bf16[2,2,2,128,128]{4,3,2,1,0:T(8,128)(2,1)S(1)} %maximum_bitcast_fusion.kv_ref, f32[64,3072]{1,0:T(8,128)S(1)} %copy-done.1, bf16[1536,1536]{1,0:T(8,128)(2,1)} %w_ref.1), custom_call_target="tpu_custom_call" | custom-call | tf_op jit(solution)/shard_map/relay_attention/pallas_call | solution.py:621
  87.8 1.1 %copy.12 = bf16[2,128,3072]{2,1,0:T(8,128)(2,1)} copy(bf16[2,128,3072]{2,1,0:T(8,128)(2,1)S(1)} %bitcast.8) | data formatting | bytes 3145728
  (1 shorter events, 0.0 us)
Async XLA Ops:
  0.0 1.3 %copy-start = (bf16[2,128,12,128]{3,1,2,0:T(8,128)(2,1)S(1)}, bf16[2,128,12,128]{3,1,2,0:T(8,128)(2,1)}, u32[]{:S(2)}) copy-start(bf16[2,128,12,128]{3,1,2,0:T(8,128)(2,1)} %param.6) | copy-start | bytes 2359300
  1.3 1.1 %copy-start.1 = (f32[64,3072]{1,0:T(8,128)S(1)}, f32[64,3072]{1,0:T(8,128)}, u32[]{:S(2)}) copy-start(f32[64,3072]{1,0:T(8,128)} %noise_hbm.1) | copy-start | bytes 2359300
  2.4 0.7 copy-start.2

commit v7 on v6

--- a/solution.py
+++ b/solution.py
@@ -17,7 +17,7 @@
     kv_send, kv_recv, kvc_send, kvc_recv, loc, wz_send, wz_recv, wf_send, wf_recv,
     wc_send, wc_recv, wy_send, wy_recv, x_send, x_recv, a_send, a_recv, c_send, c_recv, gates,
     q_ref, noise_ref, out_ref, out_sem,
-    gsend, grecv, gpart, g_send, g_recv,
+    gsend, grecv, gpart, g_send, g_recv, wl_send, wl_recv, cs_recv, xs_recv,
 ):
     y, c = lax.axis_index("rep"), lax.axis_index("span")
     z, t = lax.axis_index("seq"), lax.axis_index("tp")
@@ -44,8 +44,18 @@
     guest = z - inward
     length = jnp.where(is_end, last, last - 1) * parts
 
+    base = jnp.where(is_end, z + inward, z)
+
+    def order(k):
+        behind = both(k >= parts - 1, k < 2 * parts - 1)
+        j = jnp.where(behind, k - parts + 1, jnp.minimum(k, parts - 1))
+        return behind, j
+
     def source(e):
-        return z + inward * (e // parts + 1), e % parts
+        k = e - jnp.where(is_end, parts, 0)
+        behind, j = order(k)
+        step = jnp.where(k < 0, 0, jnp.where(behind, 2, 1))
+        return base + inward * step, jnp.where(k < 0, k + parts, j)
 
     def place(r, s, j):
         return (jnp.abs(s - r) - 1) * parts + j - keep
@@ -66,7 +76,8 @@
         return jnp.where(f < parts, f - keep, f - parts - pick)
 
     def whole(s, j):
-        return both(is_host, both(s == guest, j >= late))
+        final = both(s == z + inward, j == parts - 1)
+        return both(is_host, jnp.logical_or(both(s == guest, j >= late), final))
 
     def rows(yy, cc):
         return pl.ds(pl.multiple_of((yy * cores + cc) * quarter, quarter), quarter)
@@ -104,6 +115,12 @@
             src, wbuf.at[s, j, rows(1 - y, c)], wf_send, wf_recv.at[j], {"seq": z + inward}
         )
 
+    def final_copy():
+        src = w_ref.at[rows(1 - y, c), columns(parts - 1)]
+        return remote(
+            src, wbuf.at[z, parts - 1, rows(1 - y, c)], wl_send, wl_recv, {"seq": z + inward}
+        )
+
     def core_copy(s, j, kind):
         part = wbuf.at[s, j, rows(y if kind == 0 else 1 - y, c)]
         return remote(part, part, wc_send, wc_recv.at[turn_of(z, s, j)], {"span": 1 - c})
@@ -114,7 +131,7 @@
 
     def y_copy(s, j):
         part = wbuf.at[s, j, rows(y, c)]
-        group = jnp.where(both(is_host, s == guest), 1, 0)
+        group = jnp.where(s == guest, 1, jnp.where(s == z + 2 * inward, 2, 0))
         return remote(
             part, part, wy_send.at[group], wy_recv.at[turn_of(z, s, j)], {"rep": 1 - y}
         )
@@ -137,6 +154,21 @@
 
     def g_copy(k):
         return remote(gsend.at[k], grecv.at[k], g_send, g_recv.at[k], {"tp": 1 - t})
+
+    end_place = 2 * parts - 1 - keep
+
+    def c_part(i):
+        at = pl.ds(i * tok, tok)
+        return remote(
+            csend.at[end_place, at], cbuf.at[end_place, at], c_send, cs_recv.at[i],
+            {"seq": z - inward},
+        )
+
+    def x_part(i, at, j):
+        mine = pl.ds(i * tok, tok)
+        return remote(
+            cbuf.at[end_place, mine], xbuf.at[at, j, mine], x_send, xs_recv.at[i], {"tp": 1 - t}
+        )
 
     def kv_copy(s, g, way, own):
         dst = kvbuf.at[s, g, :, pl.ds(first, spans)]
@@ -245,7 +277,14 @@
     def pass_on(s, j):
         @pl.when(wanted(z, s, j))
         def _():
-            y_copy(s, j).wait_recv()
+            @pl.when(whole(s, j))
+            def _():
+                final_copy().wait_recv()
+
+            @pl.when(jnp.logical_not(whole(s, j)))
+            def _():
+                y_copy(s, j).wait_recv()
+
             core_copy(s, j, 1).start()
 
     def project(s, j):
@@ -275,7 +314,15 @@
         @pl.when(jnp.logical_not(add))
         def _():
             csend[f] = part.astype(jnp.bfloat16)
-            c_copy(f).start()
+
+            @pl.when(f == end_place)
+            def _():
+                for i in range(spans):
+                    c_part(i).start()
+
+            @pl.when(f != end_place)
+            def _():
+                c_copy(f).start()
 
         @pl.when(both(add, mine))
         def _():
@@ -309,11 +356,24 @@
         @pl.when(jnp.logical_not(jnp.logical_or(wanted(z, s, j), summed(z, s, j))))
         def _():
             f = place(z, s, j)
-            c_copy(f).wait_recv()
-
-            @pl.when(s // owned != t)
-            def _():
-                x_copy(s, j, cbuf.at[f]).start()
+            away = s // owned != t
+
+            @pl.when(f == end_place)
+            def _():
+                for i in range(spans):
+                    c_part(i).wait_recv()
+
+                    @pl.when(away)
+                    def _(i=i):
+                        x_part(i, lax.rem(s, owned), j).start()
+
+            @pl.when(f != end_place)
+            def _():
+                c_copy(f).wait_recv()
+
+                @pl.when(away)
+                def _():
+                    x_copy(s, j, cbuf.at[f]).start()
 
     mine = t * owned
     near = z // owned == t
@@ -321,7 +381,9 @@
     rear = 2 * mine + owned - 1 - front
 
     def finish(q):
-        s, j = jnp.where(q < parts, front, rear), lax.rem(q, parts)
+        behind, j = order(q)
+        behind = jnp.logical_or(both(near, q >= parts), both(jnp.logical_not(near), behind))
+        s, j = jnp.where(behind, rear, front), jnp.where(near, lax.rem(q, parts), j)
         at = lax.rem(s, owned)
         whole_sum = both(is_end, summed(z, s, j))
 
@@ -329,7 +391,14 @@
         def _():
             c_copy(place(z, s, j)).wait_recv()
 
-        @pl.when(jnp.logical_not(whole_sum))
+        split = both(is_end, place(z, s, j) == end_place)
+
+        @pl.when(split)
+        def _():
+            for i in range(spans):
+                x_part(i, at, j).wait_recv()
+
+        @pl.when(jnp.logical_not(jnp.logical_or(whole_sum, split)))
         def _():
             x_copy(s, j, xsend.at[at, j]).wait_recv()
 
@@ -389,7 +458,7 @@
         for g in range(kvh):
             receive(guest, g, way_in)
             receive(z + inward, g, way_out)
-        own_weights(way_in, 0, parts)
+        own_weights(way_in, 0, parts - 1)
         for g in range(kvh):
             receive(z + 2 * inward, g, way_out)
         own_weights(way_out, 0, keep)
@@ -482,7 +551,7 @@
     lax.fori_loop(0, jnp.where(is_end, parts, 0), own, 0)
 
     turn = jnp.where(c == 0, 4 * pace, 6 * pace)
-    shift, due, sums, go, own_at = 4 * pace, 9 * pace, 2 * parts, 3 * pace, 5 * pace
+    shift, due, sums, go, own_at = 3 * pace, 9 * pace, 2 * parts, 3 * pace, jnp.where(c == 0, 5 * pace, 2 * pace)
 
     def run(e, carry):
         @pl.when(both(is_end, e == go))
@@ -502,6 +571,11 @@
             @pl.when(both(k >= ahead, k < parts))
             def _():
                 arrive(guest, k, -inward)
+
+            @pl.when(k == parts - 1)
+            def _():
+                own_weights(way_in, parts - 1, parts)
+                final_copy().start()
 
         @pl.when(jnp.logical_or(is_end, e > units * pace))
         def _():
@@ -590,7 +664,9 @@
         sent(w_ref.at[piece, pl.ds(0, keep * sub)], wz_send.at[1])
         sent(wbuf.at[0, :, piece], wz_send.at[2])
         sent(wbuf.at[pl.ds(0, n - 1), :, pair], wc_send)
-        sent(wbuf.at[pl.ds(0, n - 2), :, piece], wy_send.at[0])
+        sent(wbuf.at[0, pl.ds(0, parts - 1), piece], wy_send.at[0])
+        sent(wbuf.at[0, :, piece], wy_send.at[2])
+        sent(wbuf.at[0, 0, piece], wl_send)
         sent(w_ref.at[piece, pl.ds(0, late * sub)], wy_send.at[1])
         sent(csend.at[pl.ds(0, csend.shape[0] - shared)], c_send)
         sent(gsend, g_send)
@@ -610,7 +686,7 @@
     n, tps, cores = lax.axis_size("seq"), lax.axis_size("tp"), lax.axis_size("span")
     sub, owned, wide = cols // parts, n // tps, noise_table.shape[1]
     keep, late, ahead = 4 * parts // 6, parts // 6, 4 * parts // 6
-    pick, shared = keep, parts - keep
+    pick, shared = 3 * parts // 6, parts - keep
     extra, taken = (n - 1) * parts - keep, (n - 1) * parts
     q = jnp.transpose(queries, (0, 2, 1, 3))
     kv = jnp.stack([key_states, value_states], axis=0).transpose(3, 0, 1, 2, 4)
@@ -636,7 +712,7 @@
             pltpu.VMEM((extra, spans * tok, sub), jnp.bfloat16),
             dma((2,)), dma((n, kvh)), dma, dma, dma((4,)),
             dma((3,)), dma((taken,)), dma, dma((parts,)),
-            dma, dma((taken,)), dma((2,)), dma((taken,)),
+            dma, dma((taken,)), dma((3,)), dma((taken,)),
             dma, dma((owned, parts)), dma, dma, dma, dma((extra,)),
             pltpu.VMEM((spans, 1, wide), jnp.float32),
             pltpu.VMEM(q.shape, q.dtype),
@@ -646,13 +722,13 @@
             pltpu.VMEM((shared, spans * tok, sub), jnp.bfloat16),
             pltpu.VMEM((shared, spans * tok, sub), jnp.bfloat16),
             pltpu.VMEM((shared, spans * tok, sub), jnp.float32),
-            dma, dma((shared,)),
+            dma, dma((shared,)), dma, dma, dma((spans,)), dma((spans,)),
         ],
         compiler_params=pltpu.CompilerParams(
             collective_id=0, has_side_effects=True, vmem_limit_bytes=48 * 1024 * 1024
         ),
         name="relay_attention",
-    )(plan, q, kv, noise_table, out_weight)
+    )(plan, pltpu.with_memory_space_constraint(q, pltpu.HBM), kv, pltpu.with_memory_space_constraint(noise_table, pltpu.HBM), pltpu.with_memory_space_constraint(out_weight, pltpu.HBM))
     return out.reshape(spans, tok, wide)
 
 

time: 89.6 us -> 87.8 us (0.980); the launches traced: 89 us -> 86.2 us
  Pallas kernels: 84.8 us -> 83.4 us
  local copies, waits for them, and re-layouts: 4.15 us -> 2.8 us
    pallas_call x1, Pallas kernels: 84.8 us -> 83.4 us  [fused(): pl.pallas_call(functools.partial(fused_kernel, parts, keep, late, ahead,...]
    unnamed x7 -> x3, local copies, waits for them, and re-layouts: 3.08 us -> 1.8 us
where the time goes in v7:
time: 87.8 us; the launch traced here: 86.2 us
  Pallas kernels  83.4 us (95%)
  local copies, waits for them, and re-layouts  2.8 us (3%)
    pallas_call x1, Pallas kernels, fused(): pl.pallas_call(functools.partial(fused_kernel, parts, keep, late, ahead,...  83.4 us
    unnamed x3, local copies, waits for them, and re-layouts  1.8 us

profile of v7, /device:TPU:2, one launch (start us, length us, event | category | flops | bytes accessed | tf_op | source)
XLA Modules:
  0.0 86.2 jit_solution(16590382863066676245)
XLA Ops:
  0.0 1.0 %copy_bitcast_fusion = (bf16[1,2,128,2,128]{4,2,1,0,3:T(8,128)(2,1)S(1)}, bf16[1,2,128,2,128]{4,2,1,0,3:T(8,128)(2,1)S(1)}) fusion(bf16[2,128,2,128]{3,2,1,0:T(2,128)(2,1)} %param.8, bf16[2,128,2,128]{3,2,1,0:T(2,128)(2,1)} %param.7), kind=kLoop, calls=%fused_computation.1 | loop fusion | bytes 524288 | tf_op jit(solution)/shard_map/stack | solution.py:692
  1.0 0.0 copy-start
  1.1 0.6 copy-done
  1.7 83.4 %relay_attention.1 = bf16[256,3072]{1,0:T(8,128)(2,1)S(1)} custom-call(s32[4]{0:T(128)S(1)} %copy-done, bf16[2,12,128,128]{3,2,1,0:T(8,128)(2,1)} %bitcast.9, bf16[2,2,2,128,128]{4,3,2,1,0:T(8,128)(2,1)S(1)} %maximum_bitcast_fusion.kv_ref, f32[64,3072]{1,0:T(8,128)} %noise_hbm.1, bf16[1536,1536]{1,0:T(8,128)(2,1)} %w_ref.1), custom_call_target="tpu_custom_call" | custom-call | tf_op jit(solution)/shard_map/relay_attention/pallas_call | solution.py:697
  85.1 1.1 %copy.12 = bf16[2,128,3072]{2,1,0:T(8,128)(2,1)} copy(bf16[2,128,3072]{2,1,0:T(8,128)(2,1)S(1)} %bitcast.8) | data formatting | bytes 3145728
  (1 shorter events, 0.0 us)
Async XLA Ops:
  1.0 0.7 copy-start

commit v8 on v7

--- a/solution.py
+++ b/solution.py
@@ -551,7 +551,7 @@
     lax.fori_loop(0, jnp.where(is_end, parts, 0), own, 0)
 
     turn = jnp.where(c == 0, 4 * pace, 6 * pace)
-    shift, due, sums, go, own_at = 3 * pace, 9 * pace, 2 * parts, 3 * pace, jnp.where(c == 0, 5 * pace, 2 * pace)
+    shift, due, sums, go, own_at = 3 * pace, 9 * pace, 2 * parts, 3 * pace, jnp.where(c == 0, 6 * pace, 2 * pace)
 
     def run(e, carry):
         @pl.when(both(is_end, e == go))
@@ -812,7 +812,7 @@
 
 
 def choose_parts(cols):
-    for parts in (6, 3, 2, 1):
+    for parts in (6,):
         if cols % (parts * 128) == 0:
             return parts
     return 0

time: 87.8 us -> 87.8 us (level)
  no operation moved by 1% of the time
where the time goes in v8:
time: 87.8 us; the launch traced here: 86.2 us
  Pallas kernels  83.4 us (95%)
  local copies, waits for them, and re-layouts  2.8 us (3%)
    pallas_call x1, Pallas kernels, fused(): pl.pallas_call(functools.partial(fused_kernel, parts, keep, late, ahead,...  83.4 us
    unnamed x3, local copies, waits for them, and re-layouts  1.8 us

profile of v8, /device:TPU:2, one launch (start us, length us, event | category | flops | bytes accessed | tf_op | source)
XLA Modules:
  0.0 86.2 jit_solution(2628355520501415045)
XLA Ops:
  0.0 1.0 %copy_bitcast_fusion = (bf16[1,2,128,2,128]{4,2,1,0,3:T(8,128)(2,1)S(1)}, bf16[1,2,128,2,128]{4,2,1,0,3:T(8,128)(2,1)S(1)}) fusion(bf16[2,128,2,128]{3,2,1,0:T(2,128)(2,1)} %param.8, bf16[2,128,2,128]{3,2,1,0:T(2,128)(2,1)} %param.7), kind=kLoop, calls=%fused_computation.1 | loop fusion | bytes 524288 | tf_op jit(solution)/shard_map/stack | solution.py:692
  1.0 0.0 copy-start
  1.1 0.6 copy-done
  1.7 83.4 %relay_attention.1 = bf16[256,3072]{1,0:T(8,128)(2,1)S(1)} custom-call(s32[4]{0:T(128)S(1)} %copy-done, bf16[2,12,128,128]{3,2,1,0:T(8,128)(2,1)} %bitcast.9, bf16[2,2,2,128,128]{4,3,2,1,0:T(8,128)(2,1)S(1)} %maximum_bitcast_fusion.kv_ref, f32[64,3072]{1,0:T(8,128)} %noise_hbm.1, bf16[1536,1536]{1,0:T(8,128)(2,1)} %w_ref.1), custom_call_target="tpu_custom_call" | custom-call | tf_op jit(solution)/shard_map/relay_attention/pallas_call | solution.py:697
  85.1 1.1 %copy.12 = bf16[2,128,3072]{2,1,0:T(8,128)(2,1)} copy(bf16[2,128,3072]{2,1,0:T(8,128)(2,1)S(1)} %bitcast.8) | data formatting | bytes 3145728
  (1 shorter events, 0.0 us)
Async XLA Ops:
  1.0 0.7 copy-start

commit v9 on v8

--- a/solution.py
+++ b/solution.py
@@ -207,6 +207,11 @@
     reach = ((0, z > 0), (1, z < last))
 
     barrier = pltpu.get_barrier_semaphore()
+    local_kv().start()
+    local_q().start()
+    local_noise().start()
+    for j in range(parts):
+        local_w(j).start()
     for way, ok in reach:
         @pl.when(ok)
         def _(way=way):
@@ -222,16 +227,11 @@
             @pl.when(ok)
             def _(g=g, way=way):
                 kv_copy(z, g, way, True).start()
-    local_kv().start()
 
     def own_weights(way, low, high):
         for j in range(low, high):
             z_copy(z, j, way, True).start()
 
-    local_q().start()
-    local_noise().start()
-    for j in range(parts):
-        local_w(j).start()
 
     @pl.when(is_end)
     def _():

time: 87.8 us -> 87.8 us (level)
  no operation moved by 1% of the time
where the time goes in v9:
time: 87.8 us; the launch traced here: 86.2 us
  Pallas kernels  83.4 us (95%)
  local copies, waits for them, and re-layouts  2.8 us (3%)
    pallas_call x1, Pallas kernels, fused(): pl.pallas_call(functools.partial(fused_kernel, parts, keep, late, ahead,...  83.4 us
    unnamed x3, local copies, waits for them, and re-layouts  1.8 us

profile of v9, /device:TPU:2, one launch (start us, length us, event | category | flops | bytes accessed | tf_op | source)
XLA Modules:
  0.0 86.2 jit_solution(9175177269143983960)
XLA Ops:
  0.0 1.0 %copy_bitcast_fusion = (bf16[1,2,128,2,128]{4,2,1,0,3:T(8,128)(2,1)S(1)}, bf16[1,2,128,2,128]{4,2,1,0,3:T(8,128)(2,1)S(1)}) fusion(bf16[2,128,2,128]{3,2,1,0:T(2,128)(2,1)} %param.8, bf16[2,128,2,128]{3,2,1,0:T(2,128)(2,1)} %param.7), kind=kLoop, calls=%fused_computation.1 | loop fusion | bytes 524288 | tf_op jit(solution)/shard_map/stack | solution.py:692
  1.0 0.0 copy-start
  1.1 0.6 copy-done
  1.7 83.4 %relay_attention.1 = bf16[256,3072]{1,0:T(8,128)(2,1)S(1)} custom-call(s32[4]{0:T(128)S(1)} %copy-done, bf16[2,12,128,128]{3,2,1,0:T(8,128)(2,1)} %bitcast.9, bf16[2,2,2,128,128]{4,3,2,1,0:T(8,128)(2,1)S(1)} %maximum_bitcast_fusion.kv_ref, f32[64,3072]{1,0:T(8,128)} %noise_hbm.1, bf16[1536,1536]{1,0:T(8,128)(2,1)} %w_ref.1), custom_call_target="tpu_custom_call" | custom-call | tf_op jit(solution)/shard_map/relay_attention/pallas_call | solution.py:697
  85.1 1.1 %copy.12 = bf16[2,128,3072]{2,1,0:T(8,128)(2,1)} copy(bf16[2,128,3072]{2,1,0:T(8,128)(2,1)S(1)} %bitcast.8) | data formatting | bytes 3145728
  (1 shorter events, 0.0 us)
Async XLA Ops:
  1.0 0.7 copy-start
